TPU v7x, 32 devices: a whole 2x2x4 slice. The times are simulated.
32 devices in a mesh: fourier: 2 (over x), ex: 4 (over z), ey: 4 (over y, core).
Axes of the slice: x: 2, y: 2, z: 4, core: 2. Of those that a mesh axis runs over, the one named last changes fastest.
Arguments:
- forcing: float32 [128, 81, 2048], P('fourier', None, ('ex', 'ey')), may hold values from -6 to 6
- element_coef: float32 [2048], P(('ex', 'ey')), may hold values from 0.5 to 2
- schur: float32 [128, 32, 32], P('fourier'), may hold values from -12 to 20, as said below
- couple: float32 [128, 32, 49], P('fourier'), may hold values from -0.875 to 0.875
- inner_inv: float32 [128, 49, 49], P('fourier'), may hold values from -3 to 4.5, as said below
- element_cell: int32 [2048], P(('ex', 'ey')), may hold values from 0 to 127, as said below
Outputs:
- velocity: float32 [128, 81, 2048], P('fourier', None, ('ex', 'ey'))
Inputs may be any that keep to these rules, and one draw needn't show every extreme that they name: `element_cell`: each aligned block of 128 entries is a permutation of 0 to 127. `schur`: each matrix is symmetric positive definite. `inner_inv`: each matrix is symmetric positive definite.
All inputs are finite; a program needn't handle non-finite values.
Results may differ from a plain program's by a relative error of at most 0.0001.
Values sent between devices are 32-bit elements; how exact they have to be, the bound alone decides.
A program may use at most 128 MiB of HBM per device.

v0:
```python
import math

import jax
import jax.numpy as jnp
import numpy as np
from jax import lax
from jax.sharding import PartitionSpec as P

P_SIZE = 8
NZ = 128
ITERS = 3
ELX = 8
ELY = 16


def extended(block, sides, width):
    for axis, dim in sides:
        count = lax.axis_size(axis)
        forward = [(i, i + 1) for i in range(count - 1)]
        backward = [(target, source) for source, target in forward]
        low = lax.ppermute(
            lax.slice_in_dim(block, block.shape[dim] - width, None, axis=dim), axis, forward
        )
        high = lax.ppermute(lax.slice_in_dim(block, 0, width, axis=dim), axis, backward)
        block = jnp.concatenate([low, block, high], axis=dim)
    return block


def dft_rows(length):
    row_index = jnp.arange(length)[:, None]
    plane_pos = jnp.arange(length, dtype=jnp.float32)[None, :]
    waves = ((row_index + 1) // 2).astype(jnp.float32)
    angles = 2.0 * math.pi * waves * plane_pos / length
    factor = math.sqrt(2.0 / length)
    result = jnp.where(row_index % 2 == 1, factor * jnp.cos(angles), factor * jnp.sin(angles))
    result = jnp.where(row_index == 0, 1.0 / math.sqrt(length), result)
    result = jnp.where(
        row_index == length - 1, jnp.cos(math.pi * plane_pos) / math.sqrt(length), result
    )
    return result


def node_masks(row_ids, col_ids, rows_total, cols_total):
    slots = np.arange(4 * P_SIZE)
    on_left = jnp.asarray((slots == 0) | (slots >= 3 * P_SIZE))[:, None, None]
    on_right = jnp.asarray((slots >= P_SIZE) & (slots <= 2 * P_SIZE))[:, None, None]
    on_bottom = jnp.asarray(slots <= P_SIZE)[:, None, None]
    on_top = jnp.asarray((slots >= 2 * P_SIZE) & (slots <= 3 * P_SIZE))[:, None, None]
    dropped = (
        on_left & (row_ids == 0)[None, :, None]
        | on_right & (row_ids == rows_total - 1)[None, :, None]
    )
    dropped = (
        dropped
        | on_bottom & (col_ids == 0)[None, None, :]
        | on_top & (col_ids == cols_total - 1)[None, None, :]
    )
    keep = jnp.where(dropped, 0.0, 1.0).astype(jnp.float32)
    corner_weight = jnp.asarray(np.where(slots % P_SIZE == 0, 0.25, 0.5)).astype(jnp.float32)
    return (keep, keep * corner_weight[:, None, None])


def side_lines(values):
    return (
        jnp.concatenate([values[:, 0:1], values[:, 4 * P_SIZE - 1 : 3 * P_SIZE - 1 : -1]], 1),
        values[:, P_SIZE : 2 * P_SIZE + 1],
    )


def add_sides(values, left_next, right_prev):
    blank = jnp.zeros((values.shape[0], P_SIZE - 1) + values.shape[2:], values.dtype)
    return values + jnp.concatenate(
        [right_prev[:, 0:1], blank, left_next, blank, right_prev[:, P_SIZE:0:-1]], 1
    )


def end_lines(values):
    return (values[:, 0 : P_SIZE + 1], values[:, 3 * P_SIZE : 2 * P_SIZE - 1 : -1])


def add_ends(values, bottom_next, top_prev):
    blank = jnp.zeros((values.shape[0], P_SIZE - 1) + values.shape[2:], values.dtype)
    return values + jnp.concatenate([top_prev, blank, bottom_next[:, ::-1], blank], 1)


def assemble(values):
    left_line, right_line = side_lines(values)
    padded = extended(jnp.stack([left_line, right_line], 1), (("ex", 3),), 1)
    values = add_sides(values, padded[:, 0, :, 2:, :], padded[:, 1, :, :-2, :])
    bottom_line, top_line = end_lines(values)
    padded = extended(jnp.stack([bottom_line, top_line], 1), (("ey", 4),), 1)
    return add_ends(values, padded[:, 0, :, :, 2:], padded[:, 1, :, :, :-2])


def on_device(forcing, element_coef, schur, couple, inner_inv, element_cell):
    highest = lax.Precision.HIGHEST
    modes_dev = schur.shape[0]
    node_count = forcing.shape[1]
    elements = forcing.shape[2]
    cycle_size = 4 * P_SIZE
    dft_table = dft_rows(NZ)
    own_rows = lax.dynamic_slice_in_dim(
        dft_table, lax.axis_index("fourier") * modes_dev, modes_dev, 0
    )
    columns = own_rows
    spectral = jnp.einsum(
        "mz,zne->mne",
        columns,
        lax.all_gather(forcing, "fourier", axis=0, tiled=True),
        precision=highest,
    )
    ordering = (
        jnp.zeros((elements,), jnp.int32)
        .at[element_cell]
        .set(jnp.arange(elements, dtype=jnp.int32))
    )
    gridded = jnp.take(spectral, ordering, axis=2).reshape(modes_dev, node_count, ELX, ELY)
    scaling = jnp.take(element_coef, ordering).reshape(ELX, ELY)
    row_ids = lax.axis_index("ex") * ELX + jnp.arange(ELX)
    col_ids = lax.axis_index("ey") * ELY + jnp.arange(ELY)
    keep, weights = node_masks(
        row_ids, col_ids, ELX * lax.axis_size("ex"), ELY * lax.axis_size("ey")
    )
    cycle_part = gridded[:, :cycle_size]
    inner_part = gridded[:, cycle_size:]
    condensed = cycle_part - jnp.einsum("mbi,mixy->mbxy", couple, inner_part, precision=highest)
    residual = keep * assemble(condensed)

    def operator(search):
        return keep * assemble(
            scaling * jnp.einsum("mab,mbxy->maxy", schur, search, precision=highest)
        )

    def local_sum(first, second):
        return jnp.sum(weights * first * second, axis=(1, 2, 3))

    def spread(scalars):
        return scalars[:, None, None, None]

    iterate = jnp.zeros_like(residual)

    def paired(vector, applied):
        return lax.psum((local_sum(vector, vector), local_sum(vector, applied)), ("ex", "ey"))

    applied = operator(residual)
    norm_now, curve_now = paired(residual, applied)
    step_size = norm_now / curve_now
    search = residual
    along_dir = applied
    for sweep in range(ITERS):
        iterate = iterate + spread(step_size) * search
        residual = residual - spread(step_size) * along_dir
        if sweep + 1 < ITERS:
            applied = operator(residual)
            norm_next, curve_now = paired(residual, applied)
            conj_ratio = norm_next / norm_now
            step_size = norm_next / (curve_now - conj_ratio * norm_next / step_size)
            search = residual + spread(conj_ratio) * search
            along_dir = applied + spread(conj_ratio) * along_dir
            norm_now = norm_next
    interior = jnp.einsum("mij,mjxy->mixy", inner_inv, inner_part, precision=highest) / scaling
    interior = interior - jnp.einsum("mbi,mbxy->mixy", couple, iterate, precision=highest)
    solved = jnp.concatenate([iterate, interior], 1).reshape(modes_dev, node_count, elements)
    solved = jnp.take(solved, element_cell, axis=2)
    columns = own_rows
    return lax.psum_scatter(
        jnp.einsum("mz,mne->zne", columns, solved, precision=highest),
        "fourier",
        scatter_dimension=0,
        tiled=True,
    )


def solution(mesh):
    placed = (
        P("fourier", None, ("ex", "ey")),
        P(("ex", "ey")),
        P("fourier", None, None),
        P("fourier", None, None),
        P("fourier", None, None),
        P(("ex", "ey")),
    )
    return jax.shard_map(
        on_device,
        mesh=mesh,
        in_specs=placed,
        out_specs=P("fourier", None, ("ex", "ey")),
        check_vma=False,
    )
```

profile of v0, /device:TPU:0, one launch (start us, length us, event | category | flops | bytes accessed | tf_op | source)
XLA Modules:
  0.0 861.2 jit_solution(6301851011102086025)
XLA Ops:
  12.4 68.5 %all-gather.2.cloned.1.call-done = f32[128,81,128]{2,0,1:T(8,128)} async-done(((f32[64,81,128]{2,0,1:T(8,128)}), f32[128,81,128]{2,0,1:T(8,128)}) %all-gather.2.cloned.1.call-update) | async-done | bytes 5308432 | tf_op jit(solution)/shard_map/all_gather | solution.py:109
  80.9 6.7 copy.122
  87.6 18.0 %fusion.34 = f32[64,81,128]{1,0,2:T(8,128)} fusion(f32[128,81,128]{0,1,2:T(8,128)} %copy.122, f32[128,128]{1,0:T(8,128)S(1)} %iota_multiply_fusion, s32[]{:T(128)S(6)} %select_n.78, f32[128]{0:T(128)S(1)} %cosine_multiply_fusion, pred[64]{0:T(512)(128)(4,1)S(1)} %dynamic-slice.2, pred[64]{0:T(512)(128)(4,1)S(1)} %dynamic-slice.1, ...), kind=kOutput, calls=%fused_computation.124 | convolution fusion | flops 1019265024 | bytes 7997444 | tf_op jit(solution)/shard_map/mz,zne->mne/dot_general | solution.py:106
  105.6 5.0 gather_fusion.1
  115.6 4.9 slice_subtract_fusion
  127.0 7.4 rev.48
  156.3 5.0 copy.142
  161.4 5.4 slice.276
  166.7 7.4 rev.49
  174.1 4.7 copy.143
  181.4 14.6 %concatenate.98 = f32[64,32,8,16]{1,3,2,0:T(8,128)} concatenate(f32[64,1,8,16]{1,3,2,0:T(8,128)} %bitcast.114, f32[64,7,8,16]{1,3,2,0:T(8,128)} %broadcast.299, f32[64,9,8,16]{1,3,2,0:T(8,128)} %bitcast.122, f32[64,7,8,16]{1,3,2,0:T(8,128)} %broadcast.299, f32[64,8,8,16]{1,3,2,0:T(8,128)} %rev.49), dimensions={1} | concatenate | bytes 2097152 | tf_op jit(solution)/shard_map/concatenate | solution.py:72
  200.3 4.8 slice_bitcast_fusion.6
  205.1 7.4 rev.50
  212.5 5.5 pad_maximum_fusion.48
  224.8 6.5 fusion.25
  231.3 7.4 rev.51
  238.7 8.9 %fusion.11 = f32[64,32,8,16]{1,3,2,0:T(8,128)S(1)} fusion(f32[64,32,8,16]{1,3,2,0:T(8,128)} %copy-done.8, f32[64,7,8,16]{1,3,2,0:T(8,128)} %broadcast.299, f32[64,9,8,16]{1,3,2,0:T(8,128)} %rev.51, f32[64,9,8,16]{1,3,2,0:T(8,128)} %get-tuple-element.39, f32[32,8,16]{0,2,1:T(8,128)S(1)} %get-tuple-element.68), kind=kLoop, calls=%fused_computation.29 | loop fusion | flops 1310720 | bytes 2932736 | tf_op jit(solution)/shard_map/mul | solution.py:127
  258.4 7.3 rev.52
  287.9 4.6 copy.144
  292.5 5.4 slice.283
  297.9 7.4 rev.53
  305.3 4.6 copy.145
  309.9 14.4 %concatenate.105 = f32[64,32,8,16]{1,3,2,0:T(8,128)} concatenate(f32[64,1,8,16]{1,3,2,0:T(8,128)} %bitcast.116, f32[64,7,8,16]{1,3,2,0:T(8,128)} %broadcast.299, f32[64,9,8,16]{1,3,2,0:T(8,128)} %bitcast.123, f32[64,7,8,16]{1,3,2,0:T(8,128)} %broadcast.299, f32[64,8,8,16]{1,3,2,0:T(8,128)} %rev.53), dimensions={1} | concatenate | bytes 2097152 | tf_op jit(solution)/shard_map/concatenate | solution.py:72
  328.5 4.9 slice_bitcast_fusion.4
  333.4 7.3 rev.54
  340.7 4.8 pad_maximum_fusion.46
  345.5 7.8 collective-permute-start.6
  362.3 7.3 rev.55
  369.6 13.2 %fusion.1 = (f32[64]{0:T(128)S(1)}, f32[64]{0:T(128)S(1)}, f32[64,32,8,16]{1,3,2,0:T(8,128)}) fusion(f32[64,32,8,16]{1,3,2,0:T(8,128)} %copy-done.2, f32[32,8,16]{0,2,1:T(8,128)S(1)} %get-tuple-element.67, f32[64,32,8,16]{1,3,2,0:T(8,128)} %copy-done.10, f32[64,7,8,16]{1,3,2,0:T(8,128)} %broadcast.299, f32[64,9,8,16]{1,3,2,0:T(8,128)} %rev.55, ...), kind=kLoop, calls=%fused_computation.19 | loop fusion | flops 2621312 | bytes 3998208 | tf_op jit(solution)/shard_map/reduce_sum | solution.py:135
  382.8 37.1 %all-reduce.2 = (f32[64]{0:T(128)S(1)}, f32[64]{0:T(128)S(1)}) all-reduce(f32[64]{0:T(128)S(1)} %get-tuple-element.11, f32[64]{0:T(128)S(1)} %get-tuple-element.10), channel_id=1, replica_groups=mesh['fourier'=2,'ex'=4,'ey'=4] {'ex','ey'}, use_global_device_ids=true, to_apply=%region_2.4 | all-reduce | flops 128 | bytes 1024 | tf_op jit(solution)/shard_map/psum | solution.py:143
  434.7 7.3 rev.56
  461.9 4.8 copy.146
  466.7 5.4 slice.290
  472.1 7.4 rev.57
  479.4 4.6 copy.147
  484.1 14.5 %concatenate.112 = f32[64,32,8,16]{1,3,2,0:T(8,128)} concatenate(f32[64,1,8,16]{1,3,2,0:T(8,128)} %bitcast.118, f32[64,7,8,16]{1,3,2,0:T(8,128)} %broadcast.299, f32[64,9,8,16]{1,3,2,0:T(8,128)} %bitcast.124, f32[64,7,8,16]{1,3,2,0:T(8,128)} %broadcast.299, f32[64,8,8,16]{1,3,2,0:T(8,128)} %rev.57), dimensions={1} | concatenate | bytes 2097152 | tf_op jit(solution)/shard_map/concatenate | solution.py:72
  502.9 4.9 slice_bitcast_fusion.2
  507.8 7.4 rev.58
  515.1 5.7 pad_maximum_fusion.44
  527.1 6.3 fusion.21
  533.4 7.4 rev.59
  540.8 13.5 %fusion.3 = (f32[64]{0:T(128)S(1)}, f32[64]{0:T(128)S(1)}, f32[64,32,8,16]{1,3,2,0:T(8,128)}) fusion(f32[64,32,8,16]{1,3,2,0:T(8,128)} %copy-done.7, f32[32,8,16]{0,2,1:T(8,128)S(1)} %get-tuple-element.67, f32[64,32,8,16]{1,3,2,0:T(8,128)} %copy-done.9, f32[64,7,8,16]{1,3,2,0:T(8,128)} %broadcast.299, f32[64,9,8,16]{1,3,2,0:T(8,128)} %rev.59, ...), kind=kLoop, calls=%fused_computation.21 | loop fusion | flops 2621312 | bytes 3998208 | tf_op jit(solution)/shard_map/reduce_sum | solution.py:135
  554.3 33.5 %all-reduce.1 = (f32[64]{0:T(128)S(1)}, f32[64]{0:T(128)S(1)}) all-reduce(f32[64]{0:T(128)S(1)} %get-tuple-element.9, f32[64]{0:T(128)S(1)} %get-tuple-element.8), channel_id=1, replica_groups=mesh['fourier'=2,'ex'=4,'ey'=4] {'ex','ey'}, use_global_device_ids=true, to_apply=%region_6.8 | all-reduce | flops 128 | bytes 1024 | tf_op jit(solution)/shard_map/psum | solution.py:143
  588.4 5.4 multiply_subtract_fusion
  604.7 7.3 rev.60
  632.7 5.7 copy.148
  638.4 5.4 slice.297
  643.8 7.4 rev.61
  651.2 4.6 copy.149
  655.8 14.5 %concatenate.119 = f32[64,32,8,16]{1,3,2,0:T(8,128)} concatenate(f32[64,1,8,16]{1,3,2,0:T(8,128)} %bitcast.120, f32[64,7,8,16]{1,3,2,0:T(8,128)} %broadcast.299, f32[64,9,8,16]{1,3,2,0:T(8,128)} %bitcast.125, f32[64,7,8,16]{1,3,2,0:T(8,128)} %broadcast.299, f32[64,8,8,16]{1,3,2,0:T(8,128)} %rev.61), dimensions={1} | concatenate | bytes 2097152 | tf_op jit(solution)/shard_map/concatenate | solution.py:72
  674.6 4.9 slice_bitcast_fusion
  679.5 7.4 rev.62
  686.9 4.8 pad_maximum_fusion.42
  694.6 5.6 fusion.26
  704.4 7.4 rev.63
  711.9 11.6 %fusion.5 = (f32[64]{0:T(128)S(1)}, f32[64]{0:T(128)S(1)}) fusion(f32[64,32,8,16]{1,3,2,0:T(8,128)} %copy-done.12, f32[64,32,8,16]{1,3,2,0:T(8,128)} %copy-done.11, f32[64,7,8,16]{1,3,2,0:T(8,128)} %broadcast.299, f32[64,9,8,16]{1,3,2,0:T(8,128)} %rev.63, f32[64,9,8,16]{1,3,2,0:T(8,128)} %get-tuple-element.27, f32[32,8,16]{0,2,1:T(8,128)S(1)} %get-tuple-element.68, ...), kind=kLoop, calls=%fused_computation.23 | loop fusion | flops 2621312 | bytes 2949632 | tf_op jit(solution)/shard_map/reduce_sum | solution.py:135
  723.4 31.0 %all-reduce = (f32[64]{0:T(128)S(1)}, f32[64]{0:T(128)S(1)}) all-reduce(f32[64]{0:T(128)S(1)} %get-tuple-element.7, f32[64]{0:T(128)S(1)} %get-tuple-element.6), channel_id=1, replica_groups=mesh['fourier'=2,'ex'=4,'ey'=4] {'ex','ey'}, use_global_device_ids=true, to_apply=%region_10.12 | all-reduce | flops 128 | bytes 1024 | tf_op jit(solution)/shard_map/psum | solution.py:143
  754.5 5.6 multiply_add_fusion
  760.7 4.7 subtract_bitcast_fusion
  766.5 4.5 copy.120
  771.0 5.0 gather_fusion.2
  776.0 4.5 select_bitcast_fusion
  784.5 6.6 fusion.32
  791.2 62.9 %reduce-scatter.2.cloned.1.call-done = f32[64,81,128]{2,0,1:T(8,128)} async-done(((f32[128,81,128]{2,0,1:T(8,128)}), f32[64,81,128]{2,0,1:T(8,128)}) %reduce-scatter.2.cloned.1.call-update) | async-done | bytes 2654224 | tf_op jit(solution)/shard_map/reduce_scatter | solution.py:166
  (217 shorter events, 192.9 us)
Async XLA Ops:
  6.5 4.3 copy-start
  6.5 5.6 copy-start.49
  6.5 5.7 copy-start.48
  6.5 74.4 %all-gather.2.cloned.1.call-start = ((), (), s32[]{:S(2)}) async-start(), calls=%async_computation.1 | async-start | bytes 7962624 | tf_op jit(solution)/shard_map/all_gather | solution.py:109
  7.3 846.9 %reduce-scatter.2.cloned.1.call-start = ((), (), s32[]{:S(2)}) async-start(), calls=%async_computation.2 | async-start | bytes 7962624 | tf_op jit(solution)/shard_map/reduce_scatter | solution.py:166
  7.4 80.2 %copy-start.27 = (pred[64]{0:T(512)(128)(4,1)}, pred[64]{0:T(512)(128)(4,1)S(1)}, u32[]{:S(2)}) copy-start(pred[64]{0:T(512)(128)(4,1)S(1)} %dynamic-slice) | copy-start | bytes 196
  7.5 80.1 %copy-start.29 = (pred[64]{0:T(512)(128)(4,1)}, pred[64]{0:T(512)(128)(4,1)S(1)}, u32[]{:S(2)}) copy-start(pred[64]{0:T(512)(128)(4,1)S(1)} %dynamic-slice.1) | copy-start | bytes 196
  7.6 80.0 %copy-start.31 = (pred[64]{0:T(512)(128)(4,1)}, pred[64]{0:T(512)(128)(4,1)S(1)}, u32[]{:S(2)}) copy-start(pred[64]{0:T(512)(128)(4,1)S(1)} %dynamic-slice.2) | copy-start | bytes 196
  9.7 105.9 %copy-start.19 = (f32[64,32,49,1]{2,1,3,0:T(8,128)}, f32[64,32,49,1]{2,1,3,0:T(8,128)S(1)}, u32[]{:S(2)}) copy-start(f32[64,32,49,1]{2,1,3,0:T(8,128)S(1)} %copy.124) | copy-start | bytes 1204228
  12.1 75.5 %copy-start.33 = (f32[128]{0:T(128)}, f32[128]{0:T(128)S(1)}, u32[]{:S(2)}) copy-start(f32[128]{0:T(128)S(1)} %cosine_multiply_fusion) | copy-start | bytes 1540
  12.4 75.2 %copy-start.25 = (f32[128,128]{1,0:T(8,128)}, f32[128,128]{1,0:T(8,128)S(1)}, u32[]{:S(2)}) copy-start(f32[128,128]{1,0:T(8,128)S(1)} %iota_multiply_fusion) | copy-start | bytes 196612
  115.6 4.9 copy-start.15
  141.9 8.6 copy-start.46
  141.9 8.6 %copy-start.47 = (pred[32]{0:T(512)(128)(4,1)S(1)}, pred[32]{0:T(512)(128)(4,1)}, u32[]{:S(2)}) copy-start(pred[32]{0:T(512)(128)(4,1)} %constant.113.clone) | copy-start | bytes 100
  145.8 6.3 collective-permute-start
  149.2 7.0 collective-permute-start.1
  200.3 4.8 copy-start.8
  212.5 8.2 copy-start.38
  212.5 8.3 copy-start.24
  218.0 3.7 collective-permute-start.2
  219.3 5.5 collective-permute-start.3
  220.7 320.1 %copy-start.22 = (f32[32,8,16]{0,2,1:T(8,128)}, f32[32,8,16]{0,2,1:T(8,128)S(1)}, u32[]{:S(2)}) copy-start(f32[32,8,16]{0,2,1:T(8,128)S(1)} %get-tuple-element.67) | copy-start | bytes 49156
  247.6 4.4 copy-start.2
  277.3 6.1 collective-permute-start.4
  280.7 7.0 collective-permute-start.5
  328.4 4.9 copy-start.10
  340.7 17.2 %copy-start.14 = (f32[64,9,8,16]{1,3,2,0:T(8,128)S(1)}, f32[64,9,8,16]{1,3,2,0:T(8,128)}, u32[]{:S(2)}) copy-start(f32[64,9,8,16]{1,3,2,0:T(8,128)} %rev.54) | copy-start | bytes 884740
  340.7 17.2 %copy-start.18 = (f32[64,1,9,8,16]{2,4,3,0,1:T(8,128)S(1)}, f32[64,1,9,8,16]{2,4,3,0,1:T(8,128)}, u32[]{:S(2)}) copy-start(f32[64,1,9,8,16]{2,4,3,0,1:T(8,128)} %get-tuple-element.47) | copy-start | bytes 884740
  345.5 9.3 %collective-permute-start.6 = (f32[64,2,9,8,1]{2,4,3,0,1:T(1,128)S(1)}, f32[64,2,9,8,1]{2,4,3,0,1:T(1,128)S(1)}, u32[]{:S(2)}, u32[]{:S(2)}) collective-permute-start(f32[64,2,9,8,1]{2,4,3,0,1:T(1,128)S(1)} %get-tuple-element.37), channel_id=1, source_target_pairs={{0,1},{1,2},{2,3},{4,5},{5,6},{6,7},{8,9},{9,10},{10,11},{12,13},{... | collective-permute-start | bytes 110600 | tf_op jit(solution)/shard_map/ppermute | solution.py:21
  353.3 4.5 collective-permute-start.7
  419.8 4.0 copy-start.42
  419.8 4.0 copy-start.44
  423.8 4.4 copy-start.7
  453.4 4.0 collective-permute-start.8
  454.7 7.0 collective-permute-start.9
  502.9 4.9 copy-start.9
  515.1 8.3 copy-start.51
  520.8 6.3 collective-permute-start.10
  522.1 5.0 collective-permute-start.11
  540.8 47.0 %copy-start.43 = (f32[64]{0:T(128)S(1)}, f32[64]{0:T(128)}, u32[]{:S(2)}) copy-start(f32[64]{0:T(128)} %copy-done.42) | copy-start | bytes 772
  540.8 47.0 %copy-start.45 = (f32[64]{0:T(128)S(1)}, f32[64]{0:T(128)}, u32[]{:S(2)}) copy-start(f32[64]{0:T(128)} %copy-done.44) | copy-start | bytes 772
  587.8 6.0 copy-start.35
  593.8 4.4 copy-start.12
  619.5 6.5 copy-start.41
  623.4 4.0 collective-permute-start.12
  624.7 7.0 collective-permute-start.13
  674.6 4.9 copy-start.11
  686.9 7.7 copy-start.16
  691.7 8.5 collective-permute-start.14
  693.0 7.2 copy-start.13
  693.0 7.2 copy-start.17
  693.0 7.2 collective-permute-start.15
  704.4 7.4 copy-start.23
  711.8 42.6 %copy-start.36 = (f32[64]{0:T(128)S(1)}, f32[64]{0:T(128)}, u32[]{:S(2)}) copy-start(f32[64]{0:T(128)} %copy-done.35) | copy-start | bytes 772
  711.8 42.6 %copy-start.37 = (f32[64]{0:T(128)S(1)}, f32[64]{0:T(128)}, u32[]{:S(2)}) copy-start(f32[64]{0:T(128)} %get-tuple-element.21) | copy-start | bytes 772
  754.5 5.7 copy-start.20
  754.5 6.2 copy-start.21
  771.0 5.0 copy-start.39
  780.5 4.0 copy-start.26
  780.5 4.0 copy-start.28
  780.5 4.0 copy-start.30
  780.5 4.0 copy-start.32
  780.5 4.0 copy-start.34
  784.5 69.6 %copy-start.1 = (f32[128]{0:T(128)S(1)}, f32[128]{0:T(128)}, u32[]{:S(2)}) copy-start(f32[128]{0:T(128)} %param.14) | copy-start | bytes 1540
  (6 other events, 17.4 us)
Sparse Core Ops, SparseCore 0:
  8.9 71.9 all-gather.1
  791.3 62.7 reduce-scatter.1
where the time goes:
time: 868 us; the launch traced here: 861 us
  local copies, waits for them, and re-layouts  366 us (42%)
  waiting for transfers between devices  161 us (19%)
  other arithmetic  133 us (15%)
  blocking collectives  102 us (12%)
  matrix products  52.8 us (6%)
  starting transfers between devices  31.8 us (4%)
  between operations  14.8 us (2%)
    psum x3, blocking collectives, paired(): lax.psum((local_sum(vector, vector), local_sum(vector, applied)), ('ex',...  102 us
    all_gather x1, waiting for transfers between devices, on_device(): lax.all_gather(forcing, 'fourier', axis=0, tiled=True)  68.5 us
    reduce_scatter x1, waiting for transfers between devices, on_device(): lax.psum_scatter(jnp.einsum('mz,mne->zne', columns, solved, precision=hig...  62.9 us
    concatenate x4, local copies, waits for them, and re-layouts, add_sides(): jnp.concatenate([right_prev[:, 0:1], blank, left_next, blank, right_prev[...  58 us
    unnamed x115, local copies, waits for them, and re-layouts  45.5 us
    rev x8, local copies, waits for them, and re-layouts, side_lines(): values[:, 4 * P_SIZE - 1:3 * P_SIZE - 1:-1]  44.7 us
    reduce_sum x3, other arithmetic, local_sum(): return jnp.sum(weights * first * second, axis=(1, 2, 3))  38.3 us
    rev x4, local copies, waits for them, and re-layouts, add_sides(): right_prev[:, P_SIZE:0:-1]  29.5 us
  transfers between devices with their start and end apart: 18, of which 13 were waited for; matrix products, arithmetic and copies ran while one was open for 2% of the time, Pallas kernels for 0%

commit v1 on v0

v1 whole, which is shorter than its diff:
```python
import math

import jax
import jax.numpy as jnp
import numpy as np
from jax import lax
from jax.sharding import PartitionSpec as P

P_SIZE = 8
ITERS = 3
ELX = 8
ELY = 16
NB = 4 * P_SIZE
HIGH = lax.Precision.HIGH
HIGHEST = lax.Precision.HIGHEST


def dft_rows(length):
    row_index = jnp.arange(length)[:, None]
    plane_pos = jnp.arange(length, dtype=jnp.float32)[None, :]
    waves = ((row_index + 1) // 2).astype(jnp.float32)
    angles = 2.0 * math.pi * waves * plane_pos / length
    factor = math.sqrt(2.0 / length)
    result = jnp.where(row_index % 2 == 1, factor * jnp.cos(angles), factor * jnp.sin(angles))
    result = jnp.where(row_index == 0, 1.0 / math.sqrt(length), result)
    result = jnp.where(
        row_index == length - 1, jnp.cos(math.pi * plane_pos) / math.sqrt(length), result
    )
    return result


def node_masks():
    slots = np.arange(NB)[:, None]
    cells = jnp.arange(ELX * ELY)[None, :]
    row_ids = lax.axis_index("ex") * ELX + cells // ELY
    col_ids = lax.axis_index("ey") * ELY + cells % ELY
    rows_total = ELX * lax.axis_size("ex")
    cols_total = ELY * lax.axis_size("ey")
    on_left = jnp.asarray((slots == 0) | (slots >= 3 * P_SIZE))
    on_right = jnp.asarray((slots >= P_SIZE) & (slots <= 2 * P_SIZE))
    on_bottom = jnp.asarray(slots <= P_SIZE)
    on_top = jnp.asarray((slots >= 2 * P_SIZE) & (slots <= 3 * P_SIZE))
    dropped = (
        on_left & (row_ids == 0)
        | on_right & (row_ids == rows_total - 1)
        | on_bottom & (col_ids == 0)
        | on_top & (col_ids == cols_total - 1)
    )
    keep = jnp.where(dropped, 0.0, 1.0).astype(jnp.float32)
    corner_weight = jnp.asarray(np.where(slots % P_SIZE == 0, 0.25, 0.5).astype(np.float32))
    return keep, keep * corner_weight


def shift_pair(axis):
    count = lax.axis_size(axis)
    forward = [(i, i + 1) for i in range(count - 1)]
    return forward, [(b, a) for a, b in forward]


def assemble(values):
    modes = values.shape[0]
    forward, backward = shift_pair("ex")
    left = jnp.concatenate([values[:, 0:1], values[:, NB - 1 : 3 * P_SIZE - 1 : -1]], 1)
    right = values[:, P_SIZE : 2 * P_SIZE + 1]
    low = lax.ppermute(right[:, :, -ELY:], "ex", forward)
    high = lax.ppermute(left[:, :, :ELY], "ex", backward)
    left_next = jnp.concatenate([left[:, :, ELY:], high], 2)
    right_prev = jnp.concatenate([low, right[:, :, :-ELY]], 2)
    blank = jnp.zeros((modes, P_SIZE - 1, values.shape[2]), values.dtype)
    values = values + jnp.concatenate(
        [right_prev[:, 0:1], blank, left_next, blank, right_prev[:, P_SIZE:0:-1]], 1
    )
    forward, backward = shift_pair("ey")
    bottom = values[:, 0 : P_SIZE + 1]
    top = values[:, 3 * P_SIZE : 2 * P_SIZE - 1 : -1]
    low = lax.ppermute(top[:, :, ELY - 1 :: ELY], "ey", forward)
    high = lax.ppermute(bottom[:, :, 0::ELY], "ey", backward)
    column = jnp.arange(ELX * ELY) % ELY
    bottom_next = jnp.where(
        column == ELY - 1, jnp.repeat(high, ELY, axis=2), jnp.roll(bottom, -1, axis=2)
    )
    top_prev = jnp.where(column == 0, jnp.repeat(low, ELY, axis=2), jnp.roll(top, 1, axis=2))
    return values + jnp.concatenate([top_prev, blank, bottom_next[:, ::-1], blank], 1)


def conjugate_gradients(condensed, schur, scaling):
    keep, weights = node_masks()

    def operator(search):
        return keep * assemble(
            scaling * jnp.einsum("mab,mbc->mac", schur, search, precision=HIGH)
        )

    def paired(vector, applied):
        return lax.psum(
            jnp.stack(
                [
                    jnp.sum(weights * vector * vector, axis=(1, 2)),
                    jnp.sum(weights * vector * applied, axis=(1, 2)),
                ]
            ),
            ("ex", "ey"),
        )

    def spread(scalars):
        return scalars[:, None, None]

    residual = keep * assemble(condensed)
    iterate = jnp.zeros_like(residual)
    applied = operator(residual)
    norm_now, curve_now = paired(residual, applied)
    step_size = norm_now / curve_now
    search = residual
    along_dir = applied
    for sweep in range(ITERS):
        iterate = iterate + spread(step_size) * search
        if sweep + 1 < ITERS:
            residual = residual - spread(step_size) * along_dir
            applied = operator(residual)
            norm_next, curve_now = paired(residual, applied)
            conj_ratio = norm_next / norm_now
            step_size = norm_next / (curve_now - conj_ratio * norm_next / step_size)
            search = residual + spread(conj_ratio) * search
            along_dir = applied + spread(conj_ratio) * along_dir
            norm_now = norm_next
    return iterate


def on_device(forcing, element_coef, schur, couple, inner_inv, element_cell):
    modes_dev = schur.shape[0]
    planes_dev = forcing.shape[0]
    elements = forcing.shape[2]
    groups = lax.axis_size("fourier")
    me = lax.axis_index("fourier")
    dft_table = dft_rows(modes_dev * groups)
    swap = [[(i, (i + hop) % groups) for i in range(groups)] for hop in range(groups)]
    plane_of = lambda group: lax.dynamic_slice_in_dim(dft_table, group * planes_dev, planes_dev, 1)
    rows_of = lambda table, group: lax.dynamic_slice_in_dim(table, group * modes_dev, modes_dev, 0)

    own_planes = plane_of(me)
    one_hot = (element_cell[:, None] == jnp.arange(elements)[None, :]).astype(jnp.float32)
    scaling = jnp.einsum("e,ec->c", element_coef, one_hot, precision=HIGHEST)

    order = [(me - hop) % groups for hop in range(groups)]
    couples = [couple] + [lax.ppermute(couple, "fourier", swap[h]) for h in range(1, groups)]

    partial = []
    condensed = None
    for hop in range(groups):
        spec = jnp.einsum(
            "mz,zne->mne", rows_of(own_planes, order[hop]), forcing, precision=HIGH
        )
        partial.append(spec[:, NB:])
        term = spec[:, :NB] - jnp.einsum("mbi,mie->mbe", couples[hop], spec[:, NB:], precision=HIGH)
        if hop:
            term = lax.ppermute(term, "fourier", [(b, a) for a, b in swap[hop]])
        condensed = term if condensed is None else condensed + term

    condensed = jnp.einsum("mbe,ec->mbc", condensed, one_hot, precision=HIGH)
    iterate = conjugate_gradients(condensed, schur, scaling)
    iterate = jnp.einsum("mbc,ec->mbe", iterate, one_hot, precision=HIGH)

    inner_forcing = forcing[:, NB:]
    others = [None] + [lax.ppermute(inner_forcing, "fourier", swap[h]) for h in range(1, groups)]
    velocity = None
    for hop in range(groups):
        inverse = lax.ppermute(inner_inv, "fourier", swap[hop]) if hop else inner_inv
        cycle = lax.ppermute(iterate, "fourier", swap[hop]) if hop else iterate
        inner = partial[hop]
        for far in range(1, groups):
            inner = inner + jnp.einsum(
                "mz,zne->mne",
                rows_of(plane_of(order[far]), order[hop]),
                others[far],
                precision=HIGH,
            )
        interior = jnp.einsum("mij,mje->mie", inverse, inner, precision=HIGH) / element_coef
        interior = interior - jnp.einsum("mbi,mbe->mie", couples[hop], cycle, precision=HIGH)
        term = jnp.einsum(
            "mz,mne->zne",
            rows_of(own_planes, order[hop]),
            jnp.concatenate([cycle, interior], 1),
            precision=HIGH,
        )
        velocity = term if velocity is None else velocity + term
    return velocity


def solution(mesh):
    placed = (
        P("fourier", None, ("ex", "ey")),
        P(("ex", "ey")),
        P("fourier", None, None),
        P("fourier", None, None),
        P("fourier", None, None),
        P(("ex", "ey")),
    )
    return jax.shard_map(
        on_device,
        mesh=mesh,
        in_specs=placed,
        out_specs=P("fourier", None, ("ex", "ey")),
        check_vma=False,
    )
```

time: 868 us -> 543 us (0.63)
  local copies, waits for them, and re-layouts: 366 us -> 157 us
  other arithmetic: 133 us -> 56.8 us
  waiting for transfers between devices: 161 us -> 130 us
  starting transfers between devices: 31.8 us -> 59.5 us
  matrix products: 52.8 us -> 39 us
  between operations: 14.8 us -> 1.39 us
  blocking collectives: 102 us -> 89.2 us
    rev x20 -> x12, local copies, waits for them, and re-layouts: 133 us -> 14.8 us  [the longest x4 6.81 us: assemble(): bottom_next[:, ::-1]]
    ppermute x16 -> x21, waiting for transfers between devices: 29.2 us -> 130 us  [the longest x1 52.1 us: on_device(): term = lax.ppermute(term, 'fourier', [(b, a) for a, b in swap[hop]])]
    all_gather x1 -> x0, waiting for transfers between devices: 68.5 us -> none  [on_device(): lax.all_gather(forcing, 'fourier', axis=0, tiled=True)]
    reduce_scatter x1 -> x0, waiting for transfers between devices: 62.9 us -> none  [on_device(): lax.psum_scatter(jnp.einsum('mz,mne->zne', columns, solved, precision=hig...]
    another operation x13 -> x1, local copies, waits for them, and re-layouts: 50.1 us -> 0.02 us  [the longest x8 28.1 us: assemble(): padded = extended(jnp.stack([left_line, right_line], 1), (('ex', 3),), 1)]
    concatenate x4, local copies, waits for them, and re-layouts: 58 us -> 16.6 us  [assemble(): jnp.concatenate([right_prev[:, 0:1], blank, left_next, blank, right_prev[...]
    reduce_sum x3, other arithmetic: 38.3 us -> 2.96 us  [paired(): jnp.sum(weights * vector * vector, axis=(1, 2))]
    unnamed x115 -> x93, local copies, waits for them, and re-layouts: 45.5 us -> 10.3 us
  transfers between devices with their start and end apart: 18 -> 21, of which waited for: 13 -> 11; matrix products, arithmetic and copies ran while one was open for 2% -> 39% of each run, Pallas kernels for 0% -> 0%
where the time goes in v1:
time: 543 us; the launch traced here: 533 us
  local copies, waits for them, and re-layouts  157 us (29%)
  waiting for transfers between devices  130 us (24%)
  blocking collectives  89.2 us (16%)
  starting transfers between devices  59.5 us (11%)
  other arithmetic  56.8 us (10%)
  matrix products  39 us (7%)
    psum x3, blocking collectives, paired(): lax.psum(jnp.stack([jnp.sum(weights * vector * vector, axis=(1, 2)), jnp....  89.2 us
    ppermute x1, waiting for transfers between devices, on_device(): term = lax.ppermute(term, 'fourier', [(b, a) for a, b in swap[hop]])  52.1 us
    ppermute x4, waiting for transfers between devices, assemble(): high = lax.ppermute(left[:, :, :ELY], 'ex', backward)  30.8 us
    slice x16, local copies, waits for them, and re-layouts, assemble(): jnp.roll(top, 1, axis=2)  20.8 us
    slice x8, local copies, waits for them, and re-layouts, assemble(): low = lax.ppermute(top[:, :, ELY - 1::ELY], 'ey', forward)  20.7 us
    ppermute x4, starting transfers between devices, assemble(): high = lax.ppermute(left[:, :, :ELY], 'ex', backward)  18.1 us
    concatenate x4, local copies, waits for them, and re-layouts, assemble(): jnp.concatenate([right_prev[:, 0:1], blank, left_next, blank, right_prev[...  16.6 us
    ppermute x4, waiting for transfers between devices, assemble(): low = lax.ppermute(right[:, :, -ELY:], 'ex', forward)  16.4 us
  transfers between devices with their start and end apart: 21, of which 11 were waited for; matrix products, arithmetic and copies ran while one was open for 39% of the time, Pallas kernels for 0%

profile of v1, /device:TPU:0, one launch (start us, length us, event | category | flops | bytes accessed | tf_op | source)
XLA Modules:
  0.0 533.2 jit_solution(13750129755028903267)
XLA Ops:
  0.0 3.0 collective-permute-start
  3.0 2.8 slice.357
  8.3 4.5 fusion.66
  12.8 4.5 fusion.68
  17.2 4.8 collective-permute-done
  22.0 2.1 copy.48
  27.9 2.0 collective-permute-start.1
  30.0 2.1 copy.45
  32.1 3.2 copy.51
  35.3 2.9 copy.25
  38.7 2.7 fusion.14
  41.4 10.7 %collective-permute-done.20 = f32[64,49,49]{0,2,1:T(8,128)} collective-permute-done((f32[64,49,49]{0,2,1:T(8,128)}, f32[64,49,49]{0,2,1:T(8,128)}, u32[]{:S(2)}, u32[]{:S(2)}) %collective-permute-start.20) | collective-permute-done | bytes 614688 | tf_op jit(solution)/shard_map/ppermute | solution.py:167
  52.1 4.0 copy.56
  56.1 52.1 %collective-permute-done.1 = f32[64,32,128]{2,0,1:T(8,128)} collective-permute-done((f32[64,32,128]{2,0,1:T(8,128)}, f32[64,32,128]{2,0,1:T(8,128)}, u32[]{:S(2)}, u32[]{:S(2)}) %collective-permute-start.1) | collective-permute-done | bytes 1048608 | tf_op jit(solution)/shard_map/ppermute | solution.py:156
  108.2 2.2 fusion.42
  112.3 3.8 collective-permute-start.2
  117.8 8.9 %collective-permute-done.2 = f32[64,9,16]{2,1,0:T(8,128)S(1)} collective-permute-done((f32[64,9,16]{2,1,0:T(8,128)}, f32[64,9,16]{2,1,0:T(8,128)S(1)}, u32[]{:S(2)}, u32[]{:S(2)}) %collective-permute-start.2) | collective-permute-done | bytes 36896 | tf_op jit(solution)/shard_map/ppermute | solution.py:65
  127.7 3.2 collective-permute-done.3
  133.7 2.9 slice.297
  138.9 2.1 slice.290
  141.9 3.8 collective-permute-start.4
  158.5 4.3 collective-permute-start.6
  166.3 2.0 slice_maximum_fusion.2
  168.3 14.0 %collective-permute-start.7 = (f32[64,9,16]{2,1,0:T(8,128)}, f32[64,9,16]{2,1,0:T(8,128)}, u32[]{:S(2)}, u32[]{:S(2)}) collective-permute-start(f32[64,9,16]{2,1,0:T(8,128)} %pad_maximum_fusion.10), channel_id=1, source_target_pairs={{4,0},{8,4},{12,8},{5,1},{9,5},{13,9},{6,2},{10,6},{14,10},{7,3},{... | collective-permute-start | bytes 110600 | tf_op jit(solution)/shard_map/ppermute | solution.py:66
  185.3 12.4 %collective-permute-done.7 = f32[64,9,16]{2,1,0:T(8,128)} collective-permute-done((f32[64,9,16]{2,1,0:T(8,128)}, f32[64,9,16]{2,1,0:T(8,128)}, u32[]{:S(2)}, u32[]{:S(2)}) %collective-permute-start.7) | collective-permute-done | bytes 36896 | tf_op jit(solution)/shard_map/ppermute | solution.py:66
  199.0 5.2 concatenate.102
  208.1 3.9 slice.316
  214.5 4.0 slice.309
  220.4 3.8 collective-permute-start.8
  231.6 2.2 copy.29
  233.8 2.4 maximum_select_fusion.3
  241.5 2.2 copy.27
  247.0 30.0 %psum.21 = f32[2,64]{1,0:T(2,128)S(1)} all-reduce(f32[2,64]{1,0:T(2,128)S(1)} %pad_maximum_fusion.24), channel_id=1, replica_groups=mesh['fourier'=2,'ex'=4,'ey'=4] {'ex','ey'}, use_global_device_ids=true, to_apply=%region_2.3 | all-reduce | flops 128 | bytes 1024 | tf_op jit(solution)/shard_map/psum | solution.py:95
  281.0 2.2 collective-permute-start.10
  286.8 2.0 slice_maximum_fusion.1
  290.3 3.5 collective-permute-done.10
  296.7 7.6 %collective-permute-done.11 = f32[64,9,16]{2,1,0:T(8,128)} collective-permute-done((f32[64,9,16]{2,1,0:T(8,128)}, f32[64,9,16]{2,1,0:T(8,128)}, u32[]{:S(2)}, u32[]{:S(2)}) %collective-permute-start.11) | collective-permute-done | bytes 36896 | tf_op jit(solution)/shard_map/ppermute | solution.py:66
  305.6 5.1 concatenate.109
  313.5 3.9 slice.335
  318.7 4.0 slice.328
  324.7 3.9 collective-permute-start.12
  334.7 4.1 convolution_add_fusion
  338.8 3.4 convolution_add_fusion.1
  345.8 2.2 copy.34
  348.0 2.4 maximum_select_fusion.5
  355.8 2.2 copy.32
  361.2 29.5 %psum.22 = f32[2,64]{1,0:T(2,128)S(1)} all-reduce(f32[2,64]{1,0:T(2,128)S(1)} %pad_maximum_fusion.25), channel_id=1, replica_groups=mesh['fourier'=2,'ex'=4,'ey'=4] {'ex','ey'}, use_global_device_ids=true, to_apply=%region_5.6 | all-reduce | flops 128 | bytes 1024 | tf_op jit(solution)/shard_map/psum | solution.py:95
  395.9 2.1 collective-permute-start.14
  401.4 2.0 slice_maximum_fusion
  404.9 4.0 collective-permute-done.14
  411.9 7.6 %collective-permute-done.15 = f32[64,9,16]{2,1,0:T(8,128)} collective-permute-done((f32[64,9,16]{2,1,0:T(8,128)}, f32[64,9,16]{2,1,0:T(8,128)}, u32[]{:S(2)}, u32[]{:S(2)}) %collective-permute-start.15) | collective-permute-done | bytes 36896 | tf_op jit(solution)/shard_map/ppermute | solution.py:66
  420.8 5.0 concatenate.116
  429.8 3.9 slice.354
  436.2 4.0 slice.347
  442.1 3.8 collective-permute-start.16
  453.3 2.2 copy.39
  455.6 2.4 maximum_select_fusion.7
  463.3 2.2 copy.37
  468.0 29.7 %psum.23 = f32[2,64]{1,0:T(2,128)S(1)} all-reduce(f32[2,64]{1,0:T(2,128)S(1)} %pad_maximum_fusion.26), channel_id=1, replica_groups=mesh['fourier'=2,'ex'=4,'ey'=4] {'ex','ey'}, use_global_device_ids=true, to_apply=%region_8.9 | all-reduce | flops 128 | bytes 1024 | tf_op jit(solution)/shard_map/psum | solution.py:95
  497.8 2.1 fusion.45
  501.4 2.5 fusion.8
  504.0 2.5 fusion.10
  509.6 15.3 %collective-permute-done.19 = f32[64,32,128]{2,1,0:T(8,128)S(1)} collective-permute-done((f32[64,32,128]{2,1,0:T(8,128)S(1)}, f32[64,32,128]{2,1,0:T(8,128)S(1)}, u32[]{:S(2)}, u32[]{:S(2)}) %collective-permute-start.19) | collective-permute-done | bytes 1048608 | tf_op jit(solution)/shard_map/ppermute | solution.py:168
  529.8 3.1 fusion.16
  (246 shorter events, 146.6 us)
Async XLA Ops:
  0.0 22.0 %collective-permute-start = (f32[64,32,49]{0,1,2:T(8,128)}, f32[64,32,49]{0,1,2:T(8,128)}, u32[]{:S(2)}, u32[]{:S(2)}) collective-permute-start(f32[64,32,49]{0,1,2:T(8,128)} %param.14), channel_id=1, source_target_pairs={{0,16},{16,0},{1,17},{17,1},{2,18},{18,2},{3,19},{19,3},{4,20},{20... | collective-permute-start | bytes 1204232 | tf_op jit(solution)/shard_map/ppermute | solution.py:145
  3.0 49.2 %collective-permute-start.20 = (f32[64,49,49]{0,2,1:T(8,128)}, f32[64,49,49]{0,2,1:T(8,128)}, u32[]{:S(2)}, u32[]{:S(2)}) collective-permute-start(f32[64,49,49]{0,2,1:T(8,128)} %param.15), channel_id=1, source_target_pairs={{0,16},{16,0},{1,17},{17,1},{2,18},{18,2},{3,19},{19,3},{4,20},{20... | collective-permute-start | bytes 1843976 | tf_op jit(solution)/shard_map/ppermute | solution.py:167
  5.8 328.9 %collective-permute-start.18 = (f32[64,49,128]{2,0,1:T(8,128)}, f32[64,49,128]{2,0,1:T(8,128)}, u32[]{:S(2)}, u32[]{:S(2)}) collective-permute-start(f32[64,49,128]{2,0,1:T(8,128)} %slice.357), channel_id=1, source_target_pairs={{0,16},{16,0},{1,17},{17,1},{2,18},{18,2},{3,19},{19,3},{4,20},{20... | collective-permute-start | bytes 4816904 | tf_op jit(solution)/shard_map/ppermute | solution.py:164
  17.2 6.9 %slice-start = ((f32[64,81,128]{2,0,1:T(8,128)}), f32[64,49,128]{2,0,1:T(8,128)S(1)}, s32[]{:S(2)}) async-start(f32[64,81,128]{2,0,1:T(8,128)} %fusion.66), calls=%async_computation | async-start | bytes 3211264 | tf_op jit(solution)/shard_map/slice | solution.py:154
  24.2 1.8 copy-start.10
  24.2 2.1 copy-start
  26.3 5.8 %copy-start.26 = (f32[64,49,49]{0,2,1:T(8,128)S(1)}, f32[64,49,49]{0,2,1:T(8,128)}, u32[]{:S(2)}) copy-start(f32[64,49,49]{0,2,1:T(8,128)} %param.15) | copy-start | bytes 1843972
  27.9 80.2 %collective-permute-start.1 = (f32[64,32,128]{2,0,1:T(8,128)}, f32[64,32,128]{2,0,1:T(8,128)}, u32[]{:S(2)}, u32[]{:S(2)}) collective-permute-start(f32[64,32,128]{2,0,1:T(8,128)} %slice_subtract_fusion), channel_id=1, source_target_pairs={{16,0},{0,16},{17,1},{1,17},{18,2},{2,18},{19,3},{3,19},{20,4},{4,... | collective-permute-start | bytes 3145736 | tf_op jit(solution)/shard_map/ppermute | solution.py:156
  32.1 6.6 %copy-start.12 = (f32[64,32,49]{2,1,0:T(8,128)}, f32[64,32,49]{2,1,0:T(8,128)S(1)}, u32[]{:S(2)}) copy-start(f32[64,32,49]{2,1,0:T(8,128)S(1)} %copy.45) | copy-start | bytes 1204228
  35.3 3.0 copy-start.33
  35.3 3.0 copy-start.43
  35.3 3.2 copy-start.38
  35.3 3.2 copy-start.39
  35.3 3.2 copy-start.40
  35.3 3.2 copy-start.41
  35.3 3.2 copy-start.42
  35.3 3.3 slice-start.1
  38.5 240.0 %copy-start.29 = (f32[128]{0:T(128)}, f32[128]{0:T(128)S(1)}, u32[]{:S(2)}) copy-start(f32[128]{0:T(128)S(1)} %convolution_bitcast_fusion) | copy-start | bytes 1540
  41.4 66.8 %copy-start.20 = (f32[64,128,32]{1,2,0:T(8,128)S(1)}, f32[64,128,32]{1,2,0:T(8,128)}, u32[]{:S(2)}) copy-start(f32[64,128,32]{1,2,0:T(8,128)} %fusion.14) | copy-start | bytes 3145732
  112.3 14.4 %collective-permute-start.2 = (f32[64,9,16]{2,1,0:T(8,128)}, f32[64,9,16]{2,1,0:T(8,128)S(1)}, u32[]{:S(2)}, u32[]{:S(2)}) collective-permute-start(f32[64,9,16]{2,1,0:T(8,128)} %slice.362), channel_id=1, source_target_pairs={{0,4},{4,8},{8,12},{1,5},{5,9},{9,13},{2,6},{6,10},{10,14},{3,7},{... | collective-permute-start | bytes 110600 | tf_op jit(solution)/shard_map/ppermute | solution.py:65
  116.5 14.4 %collective-permute-start.3 = (f32[64,9,16]{2,1,0:T(8,128)S(1)}, f32[64,9,16]{2,1,0:T(8,128)S(1)}, u32[]{:S(2)}, u32[]{:S(2)}) collective-permute-start(f32[64,9,16]{2,1,0:T(8,128)S(1)} %pad_maximum_fusion.11), channel_id=1, source_target_pairs={{4,0},{8,4},{12,8},{5,1},{9,5},{13,9},{6,2},{10,6},{14,10},{7,3},{... | collective-permute-start | bytes 110600 | tf_op jit(solution)/shard_map/ppermute | solution.py:66
  136.6 9.4 %collective-permute-start.5 = (f32[64,9,8]{2,1,0:T(8,128)}, f32[64,9,8]{2,1,0:T(8,128)}, u32[]{:S(2)}, u32[]{:S(2)}) collective-permute-start(f32[64,9,8]{2,1,0:T(8,128)} %slice.297), channel_id=1, source_target_pairs={{1,0},{2,1},{3,2},{5,4},{6,5},{7,6},{9,8},{10,9},{11,10},{13,12},{... | collective-permute-start | bytes 55304 | tf_op jit(solution)/shard_map/ppermute | solution.py:77
  141.9 9.1 %collective-permute-start.4 = (f32[64,9,8]{2,1,0:T(8,128)}, f32[64,9,8]{2,1,0:T(8,128)}, u32[]{:S(2)}, u32[]{:S(2)}) collective-permute-start(f32[64,9,8]{2,1,0:T(8,128)} %slice.291), channel_id=1, source_target_pairs={{0,1},{1,2},{2,3},{4,5},{5,6},{6,7},{8,9},{9,10},{10,11},{12,13},{... | collective-permute-start | bytes 55304 | tf_op jit(solution)/shard_map/ppermute | solution.py:76
  156.6 11.7 %copy-start.7 = (f32[64,32,128]{2,1,0:T(8,128)}, f32[64,32,128]{2,1,0:T(8,128)S(1)}, u32[]{:S(2)}) copy-start(f32[64,32,128]{2,1,0:T(8,128)S(1)} %fusion.23) | copy-start | bytes 3145732
  158.5 23.8 %collective-permute-start.6 = (f32[64,9,16]{2,1,0:T(8,128)}, f32[64,9,16]{2,1,0:T(8,128)}, u32[]{:S(2)}, u32[]{:S(2)}) collective-permute-start(f32[64,9,16]{2,1,0:T(8,128)} %slice.374), channel_id=1, source_target_pairs={{0,4},{4,8},{8,12},{1,5},{5,9},{9,13},{2,6},{6,10},{10,14},{3,7},{... | collective-permute-start | bytes 110600 | tf_op jit(solution)/shard_map/ppermute | solution.py:65
  168.3 29.4 %copy-start.22 = (f32[64,9,112]{2,1,0:T(8,128)S(1)}, f32[64,9,112]{2,1,0:T(8,128)}, u32[]{:S(2)}) copy-start(f32[64,9,112]{2,1,0:T(8,128)} %slice_maximum_fusion.2) | copy-start | bytes 774148
  168.3 29.4 %collective-permute-start.7 = (f32[64,9,16]{2,1,0:T(8,128)}, f32[64,9,16]{2,1,0:T(8,128)}, u32[]{:S(2)}, u32[]{:S(2)}) collective-permute-start(f32[64,9,16]{2,1,0:T(8,128)} %pad_maximum_fusion.10), channel_id=1, source_target_pairs={{4,0},{8,4},{12,8},{5,1},{9,5},{13,9},{6,2},{10,6},{14,10},{7,3},{... | collective-permute-start | bytes 110600 | tf_op jit(solution)/shard_map/ppermute | solution.py:66
  212.1 16.0 %collective-permute-start.9 = (f32[64,9,8]{2,1,0:T(8,128)}, f32[64,9,8]{2,1,0:T(8,128)}, u32[]{:S(2)}, u32[]{:S(2)}) collective-permute-start(f32[64,9,8]{2,1,0:T(8,128)} %slice.316), channel_id=1, source_target_pairs={{1,0},{2,1},{3,2},{5,4},{6,5},{7,6},{9,8},{10,9},{11,10},{13,12},{... | collective-permute-start | bytes 55304 | tf_op jit(solution)/shard_map/ppermute | solution.py:77
  220.4 17.7 %collective-permute-start.8 = (f32[64,9,8]{2,1,0:T(8,128)}, f32[64,9,8]{2,1,0:T(8,128)}, u32[]{:S(2)}, u32[]{:S(2)}) collective-permute-start(f32[64,9,8]{2,1,0:T(8,128)} %slice.310), channel_id=1, source_target_pairs={{0,1},{1,2},{2,3},{4,5},{5,6},{6,7},{8,9},{9,10},{10,11},{12,13},{... | collective-permute-start | bytes 55304 | tf_op jit(solution)/shard_map/ppermute | solution.py:76
  277.0 2.0 copy-start.31
  277.0 2.0 copy-start.36
  279.1 1.9 copy-start.8
  281.0 7.7 %copy-start.9 = (f32[64,32,128]{2,1,0:T(8,128)S(1)}, f32[64,32,128]{2,1,0:T(8,128)}, u32[]{:S(2)}) copy-start(f32[64,32,128]{2,1,0:T(8,128)} %copy-done.8) | copy-start | bytes 3145732
  281.0 12.7 %collective-permute-start.10 = (f32[64,9,16]{2,1,0:T(8,128)}, f32[64,9,16]{2,1,0:T(8,128)}, u32[]{:S(2)}, u32[]{:S(2)}) collective-permute-start(f32[64,9,16]{2,1,0:T(8,128)} %slice.386), channel_id=1, source_target_pairs={{0,4},{4,8},{8,12},{1,5},{5,9},{9,13},{2,6},{6,10},{10,14},{3,7},{... | collective-permute-start | bytes 110600 | tf_op jit(solution)/shard_map/ppermute | solution.py:65
  288.8 15.5 %copy-start.23 = (f32[64,9,112]{2,1,0:T(8,128)S(1)}, f32[64,9,112]{2,1,0:T(8,128)}, u32[]{:S(2)}) copy-start(f32[64,9,112]{2,1,0:T(8,128)} %slice_maximum_fusion.1) | copy-start | bytes 774148
  288.8 15.5 %collective-permute-start.11 = (f32[64,9,16]{2,1,0:T(8,128)}, f32[64,9,16]{2,1,0:T(8,128)}, u32[]{:S(2)}, u32[]{:S(2)}) collective-permute-start(f32[64,9,16]{2,1,0:T(8,128)} %pad_maximum_fusion.9), channel_id=1, source_target_pairs={{4,0},{8,4},{12,8},{5,1},{9,5},{13,9},{6,2},{10,6},{14,10},{7,3},{... | collective-permute-start | bytes 110600 | tf_op jit(solution)/shard_map/ppermute | solution.py:66
  317.5 24.8 %collective-permute-start.13 = (f32[64,9,8]{2,1,0:T(8,128)}, f32[64,9,8]{2,1,0:T(8,128)}, u32[]{:S(2)}, u32[]{:S(2)}) collective-permute-start(f32[64,9,8]{2,1,0:T(8,128)} %slice.335), channel_id=1, source_target_pairs={{1,0},{2,1},{3,2},{5,4},{6,5},{7,6},{9,8},{10,9},{11,10},{13,12},{... | collective-permute-start | bytes 55304 | tf_op jit(solution)/shard_map/ppermute | solution.py:77
  324.7 27.6 %collective-permute-start.12 = (f32[64,9,8]{2,1,0:T(8,128)}, f32[64,9,8]{2,1,0:T(8,128)}, u32[]{:S(2)}, u32[]{:S(2)}) collective-permute-start(f32[64,9,8]{2,1,0:T(8,128)} %slice.329), channel_id=1, source_target_pairs={{0,1},{1,2},{2,3},{4,5},{5,6},{6,7},{8,9},{9,10},{10,11},{12,13},{... | collective-permute-start | bytes 55304 | tf_op jit(solution)/shard_map/ppermute | solution.py:76
  334.7 4.1 copy-start.1
  358.0 2.5 copy-start.19
  360.5 30.2 %copy-start.32 = (f32[2,64]{1,0:T(2,128)S(1)}, f32[2,64]{1,0:T(2,128)}, u32[]{:S(2)}) copy-start(f32[2,64]{1,0:T(2,128)} %copy-done.31) | copy-start | bytes 1540
  391.3 1.9 copy-start.27
  391.3 2.0 copy-start.3
  391.3 2.0 copy-start.30
  393.2 1.8 copy-start.4
  393.9 9.6 %copy-start.6 = (f32[64,32,128]{2,1,0:T(8,128)}, f32[64,32,128]{2,1,0:T(8,128)S(1)}, u32[]{:S(2)}) copy-start(f32[64,32,128]{2,1,0:T(8,128)S(1)} %fusion.21) | copy-start | bytes 3145732
  395.9 13.1 %collective-permute-start.14 = (f32[64,9,16]{2,1,0:T(8,128)}, f32[64,9,16]{2,1,0:T(8,128)}, u32[]{:S(2)}, u32[]{:S(2)}) collective-permute-start(f32[64,9,16]{2,1,0:T(8,128)} %slice.398), channel_id=1, source_target_pairs={{0,4},{4,8},{8,12},{1,5},{5,9},{9,13},{2,6},{6,10},{10,14},{3,7},{... | collective-permute-start | bytes 110600 | tf_op jit(solution)/shard_map/ppermute | solution.py:65
  403.5 16.0 %copy-start.24 = (f32[64,9,112]{2,1,0:T(8,128)S(1)}, f32[64,9,112]{2,1,0:T(8,128)}, u32[]{:S(2)}) copy-start(f32[64,9,112]{2,1,0:T(8,128)} %slice_maximum_fusion) | copy-start | bytes 774148
  403.5 16.0 %collective-permute-start.15 = (f32[64,9,16]{2,1,0:T(8,128)}, f32[64,9,16]{2,1,0:T(8,128)}, u32[]{:S(2)}, u32[]{:S(2)}) collective-permute-start(f32[64,9,16]{2,1,0:T(8,128)} %pad_maximum_fusion.8), channel_id=1, source_target_pairs={{4,0},{8,4},{12,8},{5,1},{9,5},{13,9},{6,2},{10,6},{14,10},{7,3},{... | collective-permute-start | bytes 110600 | tf_op jit(solution)/shard_map/ppermute | solution.py:66
  433.8 16.1 %collective-permute-start.17 = (f32[64,9,8]{2,1,0:T(8,128)}, f32[64,9,8]{2,1,0:T(8,128)}, u32[]{:S(2)}, u32[]{:S(2)}) collective-permute-start(f32[64,9,8]{2,1,0:T(8,128)} %slice.354), channel_id=1, source_target_pairs={{1,0},{2,1},{3,2},{5,4},{6,5},{7,6},{9,8},{10,9},{11,10},{13,12},{... | collective-permute-start | bytes 55304 | tf_op jit(solution)/shard_map/ppermute | solution.py:77
  442.1 17.8 %collective-permute-start.16 = (f32[64,9,8]{2,1,0:T(8,128)}, f32[64,9,8]{2,1,0:T(8,128)}, u32[]{:S(2)}, u32[]{:S(2)}) collective-permute-start(f32[64,9,8]{2,1,0:T(8,128)} %slice.348), channel_id=1, source_target_pairs={{0,1},{1,2},{2,3},{4,5},{5,6},{6,7},{8,9},{9,10},{10,11},{12,13},{... | collective-permute-start | bytes 55304 | tf_op jit(solution)/shard_map/ppermute | solution.py:76
  465.5 1.7 copy-start.5
  465.5 1.8 copy-start.21
  467.3 30.4 %copy-start.35 = (f32[64]{0:T(128)S(1)}, f32[64]{0:T(128)}, u32[]{:S(2)}) copy-start(f32[64]{0:T(128)} %get-tuple-element.14) | copy-start | bytes 772
  467.3 30.4 %copy-start.28 = (f32[64]{0:T(128)S(1)}, f32[64]{0:T(128)}, u32[]{:S(2)}) copy-start(f32[64]{0:T(128)} %copy-done.27) | copy-start | bytes 772
  467.3 30.4 %copy-start.34 = (s32[128]{0:T(128)S(1)}, s32[128]{0:T(128)}, u32[]{:S(2)}) copy-start(s32[128]{0:T(128)} %param.16) | copy-start | bytes 1540
  467.3 30.4 %copy-start.37 = (f32[64]{0:T(128)S(1)}, f32[64]{0:T(128)}, u32[]{:S(2)}) copy-start(f32[64]{0:T(128)} %copy-done.36) | copy-start | bytes 772
  497.8 3.7 copy-start.14
  497.8 3.6 copy-start.17
  499.9 4.1 copy-start.15
  499.9 4.1 copy-start.16
  499.9 25.0 %collective-permute-start.19 = (f32[64,32,128]{2,1,0:T(8,128)S(1)}, f32[64,32,128]{2,1,0:T(8,128)S(1)}, u32[]{:S(2)}, u32[]{:S(2)}) collective-permute-start(f32[64,32,128]{2,1,0:T(8,128)S(1)} %fusion.45), channel_id=1, source_target_pairs={{0,16},{16,0},{1,17},{17,1},{2,18},{18,2},{3,19},{19,3},{4,20},{20... | collective-permute-start | bytes 3145736 | tf_op jit(solution)/shard_map/ppermute | solution.py:168
  507.8 17.1 %copy-start.11 = (f32[64,32,49]{2,1,0:T(8,128)S(1)}, f32[64,32,49]{2,1,0:T(8,128)}, u32[]{:S(2)}) copy-start(f32[64,32,49]{2,1,0:T(8,128)} %copy-done.10) | copy-start | bytes 1204228
  509.6 17.1 %copy-start.44 = (f32[128]{0:T(128)S(1)}, f32[128]{0:T(128)}, u32[]{:S(2)}) copy-start(f32[128]{0:T(128)} %param.12) | copy-start | bytes 1540
  (4 other events, 5.1 us)

commit v2 on v1

--- a/solution.py
+++ b/solution.py
@@ -1,9 +1,12 @@
+import functools
 import math
 
 import jax
 import jax.numpy as jnp
 import numpy as np
 from jax import lax
+from jax.experimental import pallas as pl
+from jax.experimental.pallas import tpu as pltpu
 from jax.sharding import PartitionSpec as P
 
 P_SIZE = 8
@@ -51,79 +54,299 @@
     return keep, keep * corner_weight
 
 
-def shift_pair(axis):
-    count = lax.axis_size(axis)
-    forward = [(i, i + 1) for i in range(count - 1)]
-    return forward, [(b, a) for a, b in forward]
-
-
-def assemble(values):
-    modes = values.shape[0]
-    forward, backward = shift_pair("ex")
-    left = jnp.concatenate([values[:, 0:1], values[:, NB - 1 : 3 * P_SIZE - 1 : -1]], 1)
-    right = values[:, P_SIZE : 2 * P_SIZE + 1]
-    low = lax.ppermute(right[:, :, -ELY:], "ex", forward)
-    high = lax.ppermute(left[:, :, :ELY], "ex", backward)
-    left_next = jnp.concatenate([left[:, :, ELY:], high], 2)
-    right_prev = jnp.concatenate([low, right[:, :, :-ELY]], 2)
-    blank = jnp.zeros((modes, P_SIZE - 1, values.shape[2]), values.dtype)
-    values = values + jnp.concatenate(
-        [right_prev[:, 0:1], blank, left_next, blank, right_prev[:, P_SIZE:0:-1]], 1
-    )
-    forward, backward = shift_pair("ey")
-    bottom = values[:, 0 : P_SIZE + 1]
-    top = values[:, 3 * P_SIZE : 2 * P_SIZE - 1 : -1]
-    low = lax.ppermute(top[:, :, ELY - 1 :: ELY], "ey", forward)
-    high = lax.ppermute(bottom[:, :, 0::ELY], "ey", backward)
-    column = jnp.arange(ELX * ELY) % ELY
-    bottom_next = jnp.where(
-        column == ELY - 1, jnp.repeat(high, ELY, axis=2), jnp.roll(bottom, -1, axis=2)
-    )
-    top_prev = jnp.where(column == 0, jnp.repeat(low, ELY, axis=2), jnp.roll(top, 1, axis=2))
-    return values + jnp.concatenate([top_prev, blank, bottom_next[:, ::-1], blank], 1)
-
-
-def conjugate_gradients(condensed, schur, scaling):
-    keep, weights = node_masks()
-
-    def operator(search):
-        return keep * assemble(
-            scaling * jnp.einsum("mab,mbc->mac", schur, search, precision=HIGH)
+def split_high_low(values):
+    high = lax.reduce_precision(values, 8, 7)
+    return high.astype(jnp.bfloat16), (values - high).astype(jnp.bfloat16)
+
+
+def cg_kernel(
+    modes,
+    cond_ref,
+    schur_ref,
+    scale_ref,
+    keep_ref,
+    weight_ref,
+    x_ref,
+    res_ref,
+    app_ref,
+    dir_ref,
+    along_ref,
+    xs_ref,
+    xr_ref,
+    ys_ref,
+    yr_ref,
+    ps_ref,
+    pr_ex,
+    pr_ey,
+    halo_send,
+    halo_recv,
+    sum_send_ex,
+    sum_recv_ex,
+    sum_send_ey,
+    sum_recv_ey,
+):
+    cells = cond_ref.shape[1]
+    sizes = {axis: lax.axis_size(axis) for axis in ("ex", "ey")}
+    place = {axis: lax.axis_index(axis) for axis in ("ex", "ey")}
+    lane = lax.broadcasted_iota(jnp.int32, (modes, cells), 1)
+    lane_row = lane // ELY
+    lane_col = lane % ELY
+
+    def node(n):
+        if isinstance(n, int):
+            return pl.ds(n * modes, modes)
+        return pl.ds(pl.multiple_of(n * modes, modes), modes)
+
+    def turned(value, shift):
+        shift = shift % cells
+        return pltpu.roll(value, shift, 1) if shift else value
+
+    xr_ref[...] = jnp.zeros_like(xr_ref)
+    yr_ref[...] = jnp.zeros_like(yr_ref)
+
+    barrier = pltpu.get_barrier_semaphore()
+    for axis in ("ex", "ey"):
+        for hop in range(1, sizes[axis]):
+            pl.semaphore_signal(
+                barrier,
+                inc=1,
+                device_id={axis: lax.rem(place[axis] + hop, sizes[axis])},
+                device_id_type=pl.DeviceIdType.MESH,
+            )
+    pl.semaphore_wait(barrier, sizes["ex"] + sizes["ey"] - 2)
+
+    def halo_copies(axis, send, recv, turn):
+        index = 2 * (axis == "ey")
+        up, down = [
+            pltpu.make_async_remote_copy(
+                src_ref=send.at[turn, way],
+                dst_ref=recv.at[turn, way],
+                send_sem=halo_send.at[turn, index + way],
+                recv_sem=halo_recv.at[turn, index + way],
+                device_id={axis: lax.rem(place[axis] + step + sizes[axis], sizes[axis])},
+                device_id_type=pl.DeviceIdType.MESH,
+            )
+            for way, step in ((0, 1), (1, -1))
+        ]
+        has_next = place[axis] < sizes[axis] - 1
+        has_prev = place[axis] > 0
+
+        def start():
+            pl.when(has_next)(up.start)
+            pl.when(has_prev)(down.start)
+
+        def arrive():
+            pl.when(has_prev)(up.wait_recv)
+            pl.when(has_next)(down.wait_recv)
+
+        def leave():
+            pl.when(has_next)(up.wait_send)
+            pl.when(has_prev)(down.wait_send)
+
+        return start, arrive, leave
+
+    def assemble(ref, turn):
+        left = lambda k: (NB - k) % NB
+        right = lambda k: P_SIZE + k
+        last = cells - ELY
+        up = jnp.zeros((modes, cells), jnp.float32)
+        down = up
+        for k in range(P_SIZE):
+            up = jnp.where(lane_row == k, turned(ref[node(right(k)), :], ELY * k - last), up)
+            down = jnp.where(lane_row == k, turned(ref[node(left(k)), :], ELY * k), down)
+        xs_ref[turn, 0, 0] = up
+        xs_ref[turn, 1, 0] = down
+        xs_ref[turn, 0, 1] = turned(ref[node(right(P_SIZE)), :], -last)
+        xs_ref[turn, 1, 1] = ref[node(left(P_SIZE)), :]
+        start, arrive, leave = halo_copies("ex", xs_ref, xr_ref, turn)
+        start()
+        arrive()
+        for k in range(P_SIZE + 1):
+            part, lanes = divmod(k, P_SIZE)
+            low = turned(xr_ref[turn, 0, part], -ELY * lanes)
+            high = turned(xr_ref[turn, 1, part], last - ELY * lanes)
+            here_left, here_right = ref[node(left(k)), :], ref[node(right(k)), :]
+            ref[node(left(k)), :] = here_left + jnp.where(
+                lane_row == 0, low, turned(here_right, ELY)
+            )
+            ref[node(right(k)), :] = here_right + jnp.where(
+                lane_row == ELX - 1, high, turned(here_left, -ELY)
+            )
+        leave()
+
+        bottom = lambda k: k
+        top = lambda k: 3 * P_SIZE - k
+        up = jnp.zeros((modes, cells), jnp.float32)
+        down = up
+        for k in range(P_SIZE + 1):
+            up = jnp.where(lane_col == k, turned(ref[node(top(k)), :], k - ELY + 1), up)
+            down = jnp.where(lane_col == k, turned(ref[node(bottom(k)), :], k), down)
+        ys_ref[turn, 0] = up
+        ys_ref[turn, 1] = down
+        start, arrive, leave = halo_copies("ey", ys_ref, yr_ref, turn)
+        start()
+        for n in list(range(P_SIZE + 1, 2 * P_SIZE)) + list(range(3 * P_SIZE + 1, NB)):
+            ref[node(n), :] = ref[node(n), :] * keep_ref[n : n + 1, :]
+        arrive()
+        low_all = yr_ref[turn, 0]
+        high_all = yr_ref[turn, 1]
+        for k in range(P_SIZE + 1):
+            b, t = bottom(k), top(k)
+            here_bottom, here_top = ref[node(b), :], ref[node(t), :]
+            ref[node(b), :] = keep_ref[b : b + 1, :] * (
+                here_bottom
+                + jnp.where(lane_col == 0, turned(low_all, -k), turned(here_top, 1))
+            )
+            ref[node(t), :] = keep_ref[t : t + 1, :] * (
+                here_top
+                + jnp.where(
+                    lane_col == ELY - 1, turned(high_all, ELY - 1 - k), turned(here_bottom, -1)
+                )
+            )
+        leave()
+
+    def operator(turn):
+        scale = scale_ref[0:1, :]
+        block = 8
+
+        def step(outer, carry):
+            for inner in range(block):
+                mode = outer * block + inner
+                value = res_ref[pl.ds(mode, NB, stride=modes), :]
+                high = value.astype(jnp.bfloat16)
+                low = (value - high.astype(jnp.float32)).astype(jnp.bfloat16)
+                image = jnp.dot(
+                    schur_ref[mode],
+                    jnp.concatenate([high, low, high], 0),
+                    preferred_element_type=jnp.float32,
+                )
+                app_ref[pl.ds(mode, NB, stride=modes), :] = image * scale
+            return carry
+
+        lax.fori_loop(0, modes // block, step, 0)
+        assemble(app_ref, turn)
+
+    def group_sum(mine, axis, turn, stage, slots, send_sem, recv_sem):
+        ps_ref[turn, stage] = mine
+        copies = [
+            pltpu.make_async_remote_copy(
+                src_ref=ps_ref.at[turn, stage],
+                dst_ref=slots.at[turn, hop - 1],
+                send_sem=send_sem.at[turn, hop - 1],
+                recv_sem=recv_sem.at[turn, hop - 1],
+                device_id={axis: lax.rem(place[axis] + hop, sizes[axis])},
+                device_id_type=pl.DeviceIdType.MESH,
+            )
+            for hop in range(1, sizes[axis])
+        ]
+        for copy in copies:
+            copy.start()
+        for hop, copy in enumerate(copies):
+            copy.wait_recv()
+            mine = mine + slots[turn, hop]
+        for copy in copies:
+            copy.wait_send()
+        return mine
+
+    def paired(turn):
+        def step(n, sums):
+            weighted = weight_ref[pl.ds(n, 1), :] * res_ref[node(n), :]
+            return (
+                sums[0] + weighted * res_ref[node(n), :],
+                sums[1] + weighted * app_ref[node(n), :],
+            )
+
+        zero = jnp.zeros((modes, cells), jnp.float32)
+        norm, curve = lax.fori_loop(0, NB, step, (zero, zero))
+        total = lax.dot_general(
+            jnp.ones((8, cells), jnp.float32),
+            jnp.concatenate([norm, curve], 0),
+            (((1,), (1,)), ((), ())),
+            precision=HIGHEST,
+            preferred_element_type=jnp.float32,
         )
-
-    def paired(vector, applied):
-        return lax.psum(
-            jnp.stack(
-                [
-                    jnp.sum(weights * vector * vector, axis=(1, 2)),
-                    jnp.sum(weights * vector * applied, axis=(1, 2)),
-                ]
-            ),
-            ("ex", "ey"),
+        total = group_sum(total, "ey", turn, 0, pr_ey, sum_send_ey, sum_recv_ey)
+        total = group_sum(total, "ex", turn, 1, pr_ex, sum_send_ex, sum_recv_ex)
+        row = lax.broadcasted_iota(jnp.int32, (modes, 2 * modes), 0)
+        column = lax.broadcasted_iota(jnp.int32, (modes, 2 * modes), 1)
+        pick = lambda offset: jnp.sum(
+            jnp.where(column == row + offset, total[0:1, :], 0.0), axis=1, keepdims=True
         )
-
-    def spread(scalars):
-        return scalars[:, None, None]
-
-    residual = keep * assemble(condensed)
-    iterate = jnp.zeros_like(residual)
-    applied = operator(residual)
-    norm_now, curve_now = paired(residual, applied)
-    step_size = norm_now / curve_now
-    search = residual
-    along_dir = applied
+        return pick(0), pick(modes)
+
+    res_ref[...] = cond_ref[...]
+    assemble(res_ref, 0)
+    step_size = None
     for sweep in range(ITERS):
-        iterate = iterate + spread(step_size) * search
-        if sweep + 1 < ITERS:
-            residual = residual - spread(step_size) * along_dir
-            applied = operator(residual)
-            norm_next, curve_now = paired(residual, applied)
+        operator(sweep + 1)
+        norm_next, curve_now = paired(sweep)
+        if sweep == 0:
+            conj_ratio = None
+            step_size = norm_next / curve_now
+        else:
             conj_ratio = norm_next / norm_now
             step_size = norm_next / (curve_now - conj_ratio * norm_next / step_size)
-            search = residual + spread(conj_ratio) * search
-            along_dir = applied + spread(conj_ratio) * along_dir
-            norm_now = norm_next
-    return iterate
+        norm_now = norm_next
+
+        def update(n, carry, sweep=sweep, conj_ratio=conj_ratio, step_size=step_size):
+            rows = node(n)
+            search = res_ref[rows, :]
+            if sweep:
+                search = search + conj_ratio * dir_ref[rows, :]
+                x_ref[rows, :] = x_ref[rows, :] + step_size * search
+            else:
+                x_ref[rows, :] = step_size * search
+            if sweep + 1 < ITERS:
+                dir_ref[rows, :] = search
+                along = app_ref[rows, :]
+                if sweep:
+                    along = along + conj_ratio * along_ref[rows, :]
+                along_ref[rows, :] = along
+                res_ref[rows, :] = res_ref[rows, :] - step_size * along
+            return carry
+
+        lax.fori_loop(0, NB, update, 0)
+
+
+def conjugate_gradients(condensed, schur, scaling):
+    modes, cells = condensed.shape[1:]
+    keep, weights = node_masks()
+    high, low = split_high_low(schur)
+    stacked = jnp.concatenate([high, high, low], 2)
+    field = pltpu.VMEM((NB * modes, cells), jnp.float32)
+    along_ex, along_ey = lax.axis_size("ex") - 1, lax.axis_size("ey") - 1
+    turns = ITERS + 1
+    strips = lambda *lead: pltpu.VMEM(lead + (modes, cells), jnp.float32)
+    tile = lambda *lead: pltpu.VMEM(lead + (8, 2 * modes), jnp.float32)
+    semaphores = lambda *dims: pltpu.SemaphoreType.DMA(dims)
+    whole = pl.BlockSpec(memory_space=pltpu.VMEM)
+    solved = pl.pallas_call(
+        functools.partial(cg_kernel, modes),
+        out_shape=jax.ShapeDtypeStruct((NB * modes, cells), jnp.float32),
+        in_specs=[whole] * 5,
+        out_specs=whole,
+        scratch_shapes=[field] * 4
+        + [
+            strips(turns, 2, 2),
+            strips(turns, 2, 2),
+            strips(turns, 2),
+            strips(turns, 2),
+            tile(ITERS, 2),
+            tile(ITERS, along_ex),
+            tile(ITERS, along_ey),
+            semaphores(turns, 4),
+            semaphores(turns, 4),
+            semaphores(ITERS, along_ex),
+            semaphores(ITERS, along_ex),
+            semaphores(ITERS, along_ey),
+            semaphores(ITERS, along_ey),
+        ],
+        compiler_params=pltpu.CompilerParams(
+            collective_id=0, has_side_effects=True, vmem_limit_bytes=40 << 20
+        ),
+        cost_estimate=pl.CostEstimate(flops=10**9, bytes_accessed=10**8, transcendentals=0),
+    )(condensed.reshape(NB * modes, cells), stacked, scaling[None], keep, weights)
+    return solved.reshape(NB, modes, cells)
 
 
 def on_device(forcing, element_coef, schur, couple, inner_inv, element_cell):
@@ -156,9 +379,9 @@
             term = lax.ppermute(term, "fourier", [(b, a) for a, b in swap[hop]])
         condensed = term if condensed is None else condensed + term
 
-    condensed = jnp.einsum("mbe,ec->mbc", condensed, one_hot, precision=HIGH)
+    condensed = jnp.einsum("mbe,ec->bmc", condensed, one_hot, precision=HIGH)
     iterate = conjugate_gradients(condensed, schur, scaling)
-    iterate = jnp.einsum("mbc,ec->mbe", iterate, one_hot, precision=HIGH)
+    iterate = jnp.einsum("bmc,ec->mbe", iterate, one_hot, precision=HIGH)
 
     inner_forcing = forcing[:, NB:]
     others = [None] + [lax.ppermute(inner_forcing, "fourier", swap[h]) for h in range(1, groups)]

time: 543 us -> 201 us (0.37); the launches traced: 533 us -> 200 us
  local copies, waits for them, and re-layouts: 157 us -> 21.5 us
  blocking collectives: 89.2 us -> 0 us
  Pallas kernels: 0 us -> 56.7 us
  waiting for transfers between devices: 130 us -> 73.9 us
  starting transfers between devices: 59.5 us -> 8.57 us
  other arithmetic: 56.8 us -> 6.5 us
  matrix products: 39 us -> 32.7 us
    psum x3 -> x0, blocking collectives: 89.2 us -> none  [paired(): lax.psum(jnp.stack([jnp.sum(weights * vector * vector, axis=(1, 2)), jnp....]
    slice x48 -> x0, local copies, waits for them, and re-layouts: 66.7 us -> none  [the longest x16 20.8 us: assemble(): jnp.roll(top, 1, axis=2)]
    pallas_call x0 -> x1, Pallas kernels: none -> 56.7 us  [conjugate_gradients(): pl.pallas_call(functools.partial(cg_kernel, modes), out_shape=jax.ShapeDt...]
    ppermute x16 -> x0, starting transfers between devices: 50.9 us -> none  [the longest x4 18.1 us: assemble(): high = lax.ppermute(left[:, :, :ELY], 'ex', backward)]
    ppermute x16 -> x0, waiting for transfers between devices: 47.2 us -> none  [the longest x4 30.8 us: assemble(): high = lax.ppermute(left[:, :, :ELY], 'ex', backward)]
    ppermute x1, waiting for transfers between devices: 52.1 us -> 17.6 us  [on_device(): term = lax.ppermute(term, 'fourier', [(b, a) for a, b in swap[hop]])]
    ppermute x1, waiting for transfers between devices: 10.7 us -> 42.4 us  [on_device(): lax.ppermute(inner_inv, 'fourier', swap[hop])]
    concatenate x16 -> x1, other arithmetic: 19.4 us -> 1.96 us  [conjugate_gradients(): stacked = jnp.concatenate([high, high, low], 2)]
  transfers between devices with their start and end apart: 21 -> 5, of which waited for: 11 -> 4; matrix products, arithmetic and copies ran while one was open for 39% -> 25% of each run, Pallas kernels for 0% -> 28%
where the time goes in v2:
time: 201 us; the launch traced here: 200 us
  waiting for transfers between devices  73.9 us (37%)
  Pallas kernels  56.7 us (28%)
  matrix products  32.7 us (16%)
  local copies, waits for them, and re-layouts  21.5 us (11%)
  starting transfers between devices  8.57 us (4%)
  other arithmetic  6.5 us (3%)
    pallas_call x1, Pallas kernels, conjugate_gradients(): pl.pallas_call(functools.partial(cg_kernel, modes), out_shape=jax.ShapeDt...  56.7 us
    ppermute x1, waiting for transfers between devices, on_device(): lax.ppermute(inner_inv, 'fourier', swap[hop])  42.4 us
    ppermute x1, waiting for transfers between devices, on_device(): term = lax.ppermute(term, 'fourier', [(b, a) for a, b in swap[hop]])  17.6 us
    ppermute x1, waiting for transfers between devices, on_device(): cycle = lax.ppermute(iterate, 'fourier', swap[hop]) if hop else iterate  10.8 us
    unnamed x41, local copies, waits for them, and re-layouts  10.7 us
    dot_general x2, matrix products, on_device(): jnp.einsum('mz,zne->mne', rows_of(own_planes, order[hop]), forcing, preci...  6.21 us
    dot_general x2, matrix products, on_device(): jnp.einsum('mij,mje->mie', inverse, inner, precision=HIGH) / element_coef  5.09 us
    dot_general x2, matrix products, on_device(): jnp.einsum('mz,zne->mne', rows_of(plane_of(order[far]), order[hop]), othe...  4.79 us
  transfers between devices with their start and end apart: 5, of which 4 were waited for; matrix products, arithmetic and copies ran while one was open for 25% of the time, Pallas kernels for 28%

profile of v2, /device:TPU:0, one launch (start us, length us, event | category | flops | bytes accessed | tf_op | source)
XLA Modules:
  0.0 200.2 jit_solution(9884443812655946191)
XLA Ops:
  0.0 3.0 %collective-permute-start = (f32[64,32,49]{0,1,2:T(8,128)}, f32[64,32,49]{0,1,2:T(8,128)}, u32[]{:S(2)}, u32[]{:S(2)}) collective-permute-start(f32[64,32,49]{0,1,2:T(8,128)} %param.14), channel_id=1, source_target_pairs={{0,16},{16,0},{1,17},{17,1},{2,18},{18,2},{3,19},{19,3},{4,20},{20... | collective-permute-start | bytes 1204232 | tf_op jit(solution)/shard_map/ppermute | solution.py:368
  3.0 2.8 %slice.21 = f32[64,49,128]{2,0,1:T(8,128)} slice(f32[64,81,128]{2,0,1:T(8,128)} %param.11), slice={[0:64], [32:81], [0:128]} | slice | bytes 3211264 | tf_op jit(solution)/shard_map/slice | solution.py:386
  5.8 0.1 collective-permute-start.2
  5.8 2.0 collective-permute-start.4
  7.9 0.0 copy-done.11
  7.9 1.8 copy.17
  9.7 1.8 copy.16
  11.4 0.3 select_select_fusion
  11.8 0.0 copy-start.9
  11.8 0.0 copy-start.10
  11.8 3.2 %fusion.37 = f32[64,81,128]{2,0,1:T(8,128)S(1)} fusion(f32[64,81,128]{2,0,1:T(8,128)} %param.11, f32[128,128]{1,0:T(8,128)S(1)} %select_select_fusion, s32[]{:T(128)S(6)} %select_n.138, s32[]{:T(128)S(6)} %select_n.135), kind=kOutput, calls=%fused_computation.45 | convolution fusion | flops 254803968 | bytes 5341192 | tf_op jit(solution)/shard_map/mz,zne->mne/dot_general | solution.py:373
  15.0 0.0 copy-done.9
  15.0 0.0 copy-done.10
  15.0 0.0 copy-start
  15.0 1.4 fusion.57
  16.4 0.5 copy-done
  16.8 2.0 pad_maximum_fusion.schur_ref
  18.8 0.0 copy-done.12
  18.8 0.2 fusion.30.scale_ref
  19.0 3.0 %collective-permute-done = f32[64,32,49]{0,1,2:T(8,128)} collective-permute-done((f32[64,32,49]{0,1,2:T(8,128)}, f32[64,32,49]{0,1,2:T(8,128)}, u32[]{:S(2)}, u32[]{:S(2)}) %collective-permute-start) | collective-permute-done | bytes 401440 | tf_op jit(solution)/shard_map/ppermute | solution.py:368
  22.0 2.2 %copy.25 = f32[64,32,49]{2,1,0:T(8,128)S(1)} copy(f32[64,32,49]{0,1,2:T(8,128)} %collective-permute-done) | data formatting | bytes 802816 | tf_op jit(solution)/shard_map/ppermute | solution.py:368
  24.2 0.0 copy-start.1
  24.2 1.8 fusion.12
  26.0 0.3 copy-done.1
  26.3 1.6 slice_subtract_fusion
  27.9 2.0 %collective-permute-start.1 = (f32[64,32,128]{2,0,1:T(8,128)}, f32[64,32,128]{2,0,1:T(8,128)}, u32[]{:S(2)}, u32[]{:S(2)}) collective-permute-start(f32[64,32,128]{2,0,1:T(8,128)} %slice_subtract_fusion), channel_id=1, source_target_pairs={{16,0},{0,16},{17,1},{1,17},{18,2},{2,18},{19,3},{3,19},{20,4},{4,... | collective-permute-start | bytes 3145736 | tf_op jit(solution)/shard_map/ppermute | solution.py:379
  30.0 3.0 %fusion.39 = f32[64,81,128]{2,0,1:T(8,128)S(1)} fusion(f32[64,81,128]{2,0,1:T(8,128)} %param.11, f32[128,128]{1,0:T(8,128)S(1)} %select_select_fusion, s32[]{:T(128)S(6)} %select_n.133, s32[]{:T(128)S(6)} %select_n.135), kind=kOutput, calls=%fused_computation.47 | convolution fusion | flops 254803968 | bytes 5341192 | tf_op jit(solution)/shard_map/mz,zne->mne/dot_general | solution.py:373
  33.0 3.1 %copy.22 = f32[64,32,49]{2,1,0:T(8,128)} copy(f32[64,32,49]{0,1,2:T(8,128)} %param.14) | data formatting | bytes 802816 | tf_op args[3]
  36.1 4.0 %copy.28 = f32[64,49,49]{1,2,0:T(8,128)} copy(f32[64,49,49]{0,2,1:T(8,128)} %param.15) | data formatting | bytes 1229312 | tf_op args[4]
  40.1 0.0 copy-start.17
  40.1 0.1 slice.23
  40.2 0.5 copy-done.13
  40.7 0.0 copy-done.14
  40.7 0.0 copy-done.15
  40.7 0.0 copy-done.16
  40.8 0.0 copy-done.17
  40.8 0.1 broadcast_multiply_fusion
  40.9 0.5 copy-done.5
  41.4 2.8 %fusion.14 = f32[64,128,32]{1,2,0:T(8,128)} fusion(f32[64,32,49]{2,1,0:T(8,128)S(1)} %copy-done.5, f32[64,49,128]{2,0,1:T(8,128)S(1)} %slice.23), kind=kOutput, calls=%fused_computation.14 | convolution fusion | flops 77070336 | bytes 3055616 | tf_op jit(solution)/shard_map/mbi,mie->mbe/dot_general | solution.py:377
  44.1 42.4 %collective-permute-done.4 = f32[64,49,49]{0,2,1:T(8,128)} collective-permute-done((f32[64,49,49]{0,2,1:T(8,128)}, f32[64,49,49]{0,2,1:T(8,128)}, u32[]{:S(2)}, u32[]{:S(2)}) %collective-permute-start.4) | collective-permute-done | bytes 614688 | tf_op jit(solution)/shard_map/ppermute | solution.py:390
  86.5 4.0 %copy.34 = f32[64,49,49]{1,2,0:T(8,128)} copy(f32[64,49,49]{0,2,1:T(8,128)} %collective-permute-done.4) | data formatting | bytes 1229312 | tf_op jit(solution)/shard_map/ppermute | solution.py:390
  90.5 17.6 %collective-permute-done.1 = f32[64,32,128]{2,0,1:T(8,128)} collective-permute-done((f32[64,32,128]{2,0,1:T(8,128)}, f32[64,32,128]{2,0,1:T(8,128)}, u32[]{:S(2)}, u32[]{:S(2)}) %collective-permute-start.1) | collective-permute-done | bytes 1048608 | tf_op jit(solution)/shard_map/ppermute | solution.py:379
  108.2 2.6 %fusion.22 = f32[128,64,32]{0,1,2:T(8,128)S(1)} fusion(f32[64,32,128]{2,0,1:T(8,128)} %collective-permute-done.1, f32[64,81,128]{2,0,1:T(8,128)S(1)} %fusion.39, f32[64,128,32]{1,2,0:T(8,128)} %fusion.14, s32[128]{0:T(128)S(1)} %copy-done.12), kind=kOutput, calls=%fused_computation.29 | convolution fusion | flops 201867264 | bytes 4194816 | tf_op jit(solution)/shard_map/mbe,ec->bmc/dot_general | solution.py:382
  110.7 56.7 %shard_map.109 = f32[2048,128]{1,0:T(8,128)S(1)} custom-call(f32[2048,128]{1,0:T(8,128)S(1)} %bitcast.54, bf16[64,32,96]{2,1,0:T(8,128)(2,1)S(1)} %pad_maximum_fusion.schur_ref, f32[1,128]{1,0:T(1,128)S(1)} %fusion.30.scale_ref, f32[32,128]{1,0:T(8,128)S(1)} %get-tuple-element.8.keep_ref, f32[32,128]{1,0:T(8,128)S(1)} %get-tuple-element.7.weight_ref), custom_call_target="tpu_custom_call" | custom-call | flops 1000000000 | bytes 100000000 | tf_op jit(solution)/shard_map/pallas_call | solution.py:323
  167.4 0.0 copy-start.6
  167.5 0.5 convolution_bitcast_fusion
  168.0 0.0 copy-start.2
  168.0 1.6 collective-permute-start.3
  169.6 0.0 copy-done.6
  169.6 2.0 fusion.27
  171.6 0.0 collective-permute-done.2
  171.6 2.4 %convolution_add_fusion = f32[64,49,128]{2,0,1:T(8,128)S(1)} fusion(f32[64,49,128]{2,0,1:T(8,128)} %collective-permute-done.2, f32[128,128]{1,0:T(8,128)S(1)} %select_select_fusion, s32[]{:T(128)S(6)} %select_n.138, f32[64,81,128]{2,0,1:T(8,128)S(1)} %copy-done.2), kind=kOutput, calls=%fused_computation.23 | convolution fusion | flops 154542080 | bytes 4849668 | tf_op jit(solution)/shard_map/mz,zne->mne/dot_general | solution.py:394
  174.0 2.4 %convolution_add_fusion.1 = f32[64,49,128]{2,0,1:T(8,128)S(1)} fusion(f32[64,49,128]{2,0,1:T(8,128)} %collective-permute-done.2, f32[128,128]{1,0:T(8,128)S(1)} %select_select_fusion, s32[]{:T(128)S(6)} %select_n.133, s32[]{:T(128)S(6)} %select_n.138, f32[64,81,128]{2,0,1:T(8,128)S(1)} %fusion.39), kind=kOutput, calls=%fused_computation.24 | convolution fusion | flops 154542080 | bytes 4849672 | tf_op jit(solution)/shard_map/mz,zne->mne/dot_general | solution.py:394
  176.4 0.0 copy-done.8
  176.4 0.0 copy-start.7
  176.4 2.5 %fusion.8 = f32[64,128,49]{1,2,0:T(8,128)S(1)} fusion(f32[64,49,49]{1,2,0:T(8,128)S(1)} %copy-done.8, f32[64,49,128]{2,0,1:T(8,128)S(1)} %convolution_add_fusion), kind=kOutput, calls=%fused_computation.8 | convolution fusion | flops 118013952 | bytes 3825920 | tf_op jit(solution)/shard_map/mij,mje->mie/dot_general | solution.py:400
  179.0 0.0 copy-done.7
  179.0 0.0 copy-start.4
  179.0 2.5 %fusion.10 = f32[64,128,49]{1,2,0:T(8,128)S(1)} fusion(f32[64,49,49]{1,2,0:T(8,128)S(1)} %copy-done.7, f32[64,49,128]{2,0,1:T(8,128)S(1)} %convolution_add_fusion.1), kind=kOutput, calls=%fused_computation.10 | convolution fusion | flops 118013952 | bytes 3825920 | tf_op jit(solution)/shard_map/mij,mje->mie/dot_general | solution.py:400
  181.5 10.8 %collective-permute-done.3 = f32[64,32,128]{2,0,1:T(8,128)S(1)} collective-permute-done((f32[64,32,128]{2,0,1:T(8,128)S(1)}, f32[64,32,128]{2,0,1:T(8,128)S(1)}, u32[]{:S(2)}, u32[]{:S(2)}) %collective-permute-start.3) | collective-permute-done | bytes 1048608 | tf_op jit(solution)/shard_map/ppermute | solution.py:391
  192.4 2.0 fusion.25
  194.4 1.0 fusion.19
  195.4 1.7 fusion
  197.1 3.1 %fusion.16 = f32[64,81,128]{2,0,1:T(8,128)} fusion(f32[64,81,128]{2,0,1:T(8,128)S(1)} %fusion, f32[64,49,128]{2,0,1:T(8,128)S(1)} %get-tuple-element.9, f32[64,32,128]{2,0,1:T(8,128)S(1)} %collective-permute-done.3, f32[128,128]{1,0:T(8,128)S(1)} %select_select_fusion, s32[]{:T(128)S(6)} %select_n.138, s32[]{:T(128)S(6)} %select_n.135), kind=kOutput, calls=%fused_computation.16 | convolution fusion | flops 256131072 | bytes 7995400 | tf_op jit(solution)/shard_map/mz,mne->zne/dot_general | solution.py:402
  (22 shorter events, 0.1 us)
Async XLA Ops:
  0.0 7.9 %copy-start.11 = (f32[64,32,32]{0,2,1:T(8,128)S(1)}, f32[64,32,32]{0,2,1:T(8,128)}, u32[]{:S(2)}) copy-start(f32[64,32,32]{0,2,1:T(8,128)} %param.13) | copy-start | bytes 786436
  0.0 22.0 %collective-permute-start = (f32[64,32,49]{0,1,2:T(8,128)}, f32[64,32,49]{0,1,2:T(8,128)}, u32[]{:S(2)}, u32[]{:S(2)}) collective-permute-start(f32[64,32,49]{0,1,2:T(8,128)} %param.14), channel_id=1, source_target_pairs={{0,16},{16,0},{1,17},{17,1},{2,18},{18,2},{3,19},{19,3},{4,20},{20... | collective-permute-start | bytes 1204232 | tf_op jit(solution)/shard_map/ppermute | solution.py:368
  5.8 165.8 %collective-permute-start.2 = (f32[64,49,128]{2,0,1:T(8,128)}, f32[64,49,128]{2,0,1:T(8,128)}, u32[]{:S(2)}, u32[]{:S(2)}) collective-permute-start(f32[64,49,128]{2,0,1:T(8,128)} %slice.21), channel_id=1, source_target_pairs={{0,16},{16,0},{1,17},{17,1},{2,18},{18,2},{3,19},{19,3},{4,20},{20... | collective-permute-start | bytes 4816904 | tf_op jit(solution)/shard_map/ppermute | solution.py:387
  5.8 80.7 %collective-permute-start.4 = (f32[64,49,49]{0,2,1:T(8,128)}, f32[64,49,49]{0,2,1:T(8,128)}, u32[]{:S(2)}, u32[]{:S(2)}) collective-permute-start(f32[64,49,49]{0,2,1:T(8,128)} %param.15), channel_id=1, source_target_pairs={{0,16},{16,0},{1,17},{17,1},{2,18},{18,2},{3,19},{19,3},{4,20},{20... | collective-permute-start | bytes 1843976 | tf_op jit(solution)/shard_map/ppermute | solution.py:390
  11.8 3.2 %copy-start.9 = (f32[64,32,32]{2,1,0:T(8,128)S(1)}, f32[64,32,32]{2,1,0:T(8,128)}, u32[]{:S(2)}) copy-start(f32[64,32,32]{2,1,0:T(8,128)} %copy.17) | copy-start | bytes 786436
  11.8 3.2 %copy-start.10 = (f32[64,32,32]{2,1,0:T(8,128)S(1)}, f32[64,32,32]{2,1,0:T(8,128)}, u32[]{:S(2)}) copy-start(f32[64,32,32]{2,1,0:T(8,128)} %copy.16) | copy-start | bytes 786436
  15.0 1.8 copy-start
  16.4 2.4 %copy-start.12 = (s32[128]{0:T(128)S(1)}, s32[128]{0:T(128)}, u32[]{:S(2)}) copy-start(s32[128]{0:T(128)} %param.16) | copy-start | bytes 1540
  16.4 2.4 %copy-start.18 = (f32[128]{0:T(128)S(1)}, f32[128]{0:T(128)}, u32[]{:S(2)}) copy-start(f32[128]{0:T(128)} %param.12) | copy-start | bytes 1540
  16.8 7.3 %slice-start = ((f32[64,81,128]{2,0,1:T(8,128)}), f32[64,49,128]{2,0,1:T(8,128)S(1)}, s32[]{:S(2)}) async-start(f32[64,81,128]{2,0,1:T(8,128)} %copy-done), calls=%async_computation | async-start | bytes 3211264 | tf_op jit(solution)/shard_map/slice | solution.py:377
  24.2 1.8 copy-start.3
  24.2 2.1 %copy-start.1 = (f32[64,81,128]{2,0,1:T(8,128)S(1)}, f32[64,81,128]{2,0,1:T(8,128)}, u32[]{:S(2)}) copy-start(f32[64,81,128]{2,0,1:T(8,128)} %copy-done) | copy-start | bytes 7962628
  27.9 80.2 %collective-permute-start.1 = (f32[64,32,128]{2,0,1:T(8,128)}, f32[64,32,128]{2,0,1:T(8,128)}, u32[]{:S(2)}, u32[]{:S(2)}) collective-permute-start(f32[64,32,128]{2,0,1:T(8,128)} %slice_subtract_fusion), channel_id=1, source_target_pairs={{16,0},{0,16},{17,1},{1,17},{18,2},{2,18},{19,3},{3,19},{20,4},{4,... | collective-permute-start | bytes 3145736 | tf_op jit(solution)/shard_map/ppermute | solution.py:379
  40.1 0.7 copy-start.13
  40.1 0.7 copy-start.14
  40.1 0.7 copy-start.15
  40.1 0.7 copy-start.16
  40.1 0.7 copy-start.17
  40.1 1.3 copy-start.5
  167.4 2.1 %copy-start.6 = (f32[64,32,49]{2,1,0:T(8,128)S(1)}, f32[64,32,49]{2,1,0:T(8,128)}, u32[]{:S(2)}) copy-start(f32[64,32,49]{2,1,0:T(8,128)} %copy.22) | copy-start | bytes 1204228
  168.0 3.6 %copy-start.2 = (f32[64,81,128]{2,0,1:T(8,128)S(1)}, f32[64,81,128]{2,0,1:T(8,128)}, u32[]{:S(2)}) copy-start(f32[64,81,128]{2,0,1:T(8,128)} %copy-done) | copy-start | bytes 7962628
  168.0 24.4 %collective-permute-start.3 = (f32[64,32,128]{2,0,1:T(8,128)S(1)}, f32[64,32,128]{2,0,1:T(8,128)S(1)}, u32[]{:S(2)}, u32[]{:S(2)}) collective-permute-start(f32[64,32,128]{2,0,1:T(8,128)S(1)} %convolution_bitcast_fusion), channel_id=1, source_target_pairs={{0,16},{16,0},{1,17},{17,1},{2,18},{18,2},{3,19},{19,3},{4,20},{20... | collective-permute-start | bytes 3145736 | tf_op jit(solution)/shard_map/ppermute | solution.py:391
  174.0 2.4 %copy-start.8 = (f32[64,49,49]{1,2,0:T(8,128)S(1)}, f32[64,49,49]{1,2,0:T(8,128)}, u32[]{:S(2)}) copy-start(f32[64,49,49]{1,2,0:T(8,128)} %copy.34) | copy-start | bytes 1843972
  176.4 2.6 %copy-start.7 = (f32[64,49,49]{1,2,0:T(8,128)S(1)}, f32[64,49,49]{1,2,0:T(8,128)}, u32[]{:S(2)}) copy-start(f32[64,49,49]{1,2,0:T(8,128)} %copy.28) | copy-start | bytes 1843972
  179.0 13.4 %copy-start.4 = (f32[64,32,49]{2,1,0:T(8,128)S(1)}, f32[64,32,49]{2,1,0:T(8,128)}, u32[]{:S(2)}) copy-start(f32[64,32,49]{2,1,0:T(8,128)} %copy-done.3) | copy-start | bytes 1204228
